TPU v7x, 32 devices: a whole 2x2x4 slice. The times are simulated.
32 devices in a mesh: rep: 4 (over y, core), fsdp: 8 (over z, x).
Axes of the slice: x: 2, y: 2, z: 4, core: 2. Of those that a mesh axis runs over, the one named last changes fastest.
Arguments:
- tokens: bfloat16 [32128, 768], P(('rep', 'fsdp')), may hold values from -6 to 6
- read_memory: bfloat16 [320, 768], P(('rep', 'fsdp')), may hold values from -6 to 6
- doc_ids: int32 [32, 1004], P(('rep', 'fsdp')), may hold values from 0 to 15, never falling along the last dimension, each value on 1 to 256 neighbouring positions
- w_query: bfloat16 [768, 768], P('fsdp'), may hold values from -0.21875 to 0.21875
- w_key: bfloat16 [768, 768], P('fsdp'), may hold values from -0.21875 to 0.21875
- w_value: bfloat16 [768, 768], P('fsdp'), may hold values from -0.21875 to 0.21875
- w_out: bfloat16 [768, 768], P('fsdp'), may hold values from -1.75 to 1.75
- query_bias: bfloat16 [768], P('fsdp'), may hold values from -3 to 3
- value_bias: bfloat16 [768], P('fsdp'), may hold values from -3 to 3
- out_bias: bfloat16 [768], P('fsdp'), may hold values from -3 to 3
- norm_one_gain: bfloat16 [768], P('fsdp'), may hold values from 0.099609375 to 1.8984375
- norm_one_bias: bfloat16 [768], P('fsdp'), may hold values from -3 to 3
- w_inner: bfloat16 [768, 3072], P('fsdp'), may hold values from -0.21875 to 0.21875
- inner_bias: bfloat16 [3072], P('fsdp'), may hold values from -3 to 3
- w_outer: bfloat16 [3072, 768], P('fsdp'), may hold values from -0.109375 to 0.109375
- outer_bias: bfloat16 [768], P('fsdp'), may hold values from -3 to 3
- norm_two_gain: bfloat16 [768], P('fsdp'), may hold values from 0.099609375 to 1.8984375
- norm_two_bias: bfloat16 [768], P('fsdp'), may hold values from -3 to 3
- out_grad: bfloat16 [32768, 768], P(('rep', 'fsdp')), may hold values from -6 to 6
Outputs:
- layer_out: bfloat16 [32768, 768], P(('rep', 'fsdp'))
- grad_tokens: bfloat16 [32128, 768], P(('rep', 'fsdp'))
- grad_memory: bfloat16 [320, 768], P(('rep', 'fsdp'))
- grad_w_query: float32 [768, 768], P('fsdp')
- grad_w_key: float32 [768, 768], P('fsdp')
- grad_w_value: float32 [768, 768], P('fsdp')
- grad_w_out: float32 [768, 768], P('fsdp')
- grad_query_bias: float32 [768], P('fsdp')
- grad_value_bias: float32 [768], P('fsdp')
- grad_out_bias: float32 [768], P('fsdp')
- grad_norm_one_gain: float32 [768], P('fsdp')
- grad_norm_one_bias: float32 [768], P('fsdp')
- grad_w_inner: float32 [768, 3072], P('fsdp')
- grad_inner_bias: float32 [3072], P('fsdp')
- grad_w_outer: float32 [3072, 768], P('fsdp')
- grad_outer_bias: float32 [768], P('fsdp')
- grad_norm_two_gain: float32 [768], P('fsdp')
- grad_norm_two_bias: float32 [768], P('fsdp')
Inputs may be any that keep to these rules, and one draw needn't show every extreme that they name: `doc_ids`: in each sequence the document numbers never fall, every number occurs, each document holds at most 256 tokens and one holds exactly that many.
All inputs are finite; a program needn't handle non-finite values.
Results may differ from a plain program's by a relative error of at most 0.02.
Values may be sent and summed in bfloat16 or wider, within the bound.
A program may use at most 320 MiB of HBM per device.

v0:
```python
from functools import partial

import jax
import jax.numpy as jnp
from jax import lax
from jax.sharding import PartitionSpec as P

HEADS = 12
HEAD_DIM = 64


def layer_norm(value, gain, shift):
    mean = jnp.mean(value, axis=-1, keepdims=True)
    centered = value - mean
    spread = jnp.mean(centered * centered, axis=-1, keepdims=True)
    return centered * lax.rsqrt(spread + 1e-05) * gain + shift


def product(left, right):
    return jnp.dot(left, right, preferred_element_type=jnp.float32)


def inner_rows(left, right):
    return lax.dot_general(
        left, right, (((0,), (0,)), ((), ())), preferred_element_type=jnp.float32
    )


def against(left, right):
    return lax.dot_general(
        left, right, (((1,), (1,)), ((), ())), preferred_element_type=jnp.float32
    )


def column_sum(values):
    return jnp.sum(values.astype(jnp.float32), axis=0)


def block_scores(query_block, keys, row_ids, col_ids, factor):
    scores = (
        jnp.einsum("qhd,khd->hqk", query_block, keys, preferred_element_type=jnp.float32) * factor
    )
    allowed = (
        (row_ids[:, None] == col_ids[None, :]) | (row_ids[:, None] < 0) | (col_ids[None, :] < 0)
    )
    return jnp.where(allowed[None], scores, jnp.float32(-1e30))


def attend_forward(query, keys, values, ids, factor, block):
    pieces = []
    sums = []
    for start in range(0, query.shape[0], block):
        scores = block_scores(
            query[start : start + block], keys, ids[start : start + block], ids, factor
        )
        peak = jnp.max(scores, axis=-1, keepdims=True)
        weights = jnp.exp(scores - peak)
        total = jnp.sum(weights, axis=-1, keepdims=True)
        probs = (weights / total).astype(jnp.bfloat16)
        pieces.append(jnp.einsum("hqk,khd->qhd", probs, values, preferred_element_type=jnp.float32))
        sums.append(peak + jnp.log(total))
    return (jnp.concatenate(pieces, axis=0), jnp.concatenate(sums, axis=1))


def attend_backward(query, keys, values, ids, log_sums, grad_out, factor, block):
    grad_query = []
    grad_keys = jnp.zeros(keys.shape, jnp.float32)
    grad_values = jnp.zeros(values.shape, jnp.float32)
    for start in range(0, query.shape[0], block):
        query_block = query[start : start + block]
        scores = block_scores(query_block, keys, ids[start : start + block], ids, factor)
        probs = jnp.exp(scores - log_sums[:, start : start + block])
        grad_block = grad_out[start : start + block]
        grad_values = grad_values + jnp.einsum(
            "hqk,qhd->khd",
            probs.astype(jnp.bfloat16),
            grad_block,
            preferred_element_type=jnp.float32,
        )
        grad_probs = jnp.einsum(
            "qhd,khd->hqk", grad_block, values, preferred_element_type=jnp.float32
        )
        centre = jnp.sum(probs * grad_probs, axis=-1, keepdims=True)
        grad_scores = (probs * (grad_probs - centre)).astype(jnp.bfloat16)
        grad_query.append(
            jnp.einsum("hqk,khd->qhd", grad_scores, keys, preferred_element_type=jnp.float32)
            * factor
        )
        grad_keys = (
            grad_keys
            + jnp.einsum(
                "hqk,qhd->khd", grad_scores, query_block, preferred_element_type=jnp.float32
            )
            * factor
        )
    return (jnp.concatenate(grad_query, axis=0), grad_keys, grad_values)


def on_device(
    tokens,
    read_memory,
    doc_ids,
    w_query,
    w_key,
    w_value,
    w_out,
    query_bias,
    value_bias,
    out_bias,
    norm_one_gain,
    norm_one_bias,
    w_inner,
    inner_bias,
    w_outer,
    outer_bias,
    norm_two_gain,
    norm_two_bias,
    out_grad,
):
    (
        query_mat,
        key_mat,
        value_mat,
        out_mat,
        query_shift,
        value_shift,
        out_shift,
        gain_one,
        shift_one,
        inner_mat,
        inner_shift,
        outer_mat,
        outer_shift,
        gain_two,
        shift_two,
    ) = (
        lax.all_gather(w_query, "fsdp", axis=0, tiled=True),
        lax.all_gather(w_key, "fsdp", axis=0, tiled=True),
        lax.all_gather(w_value, "fsdp", axis=0, tiled=True),
        lax.all_gather(w_out, "fsdp", axis=0, tiled=True),
        lax.all_gather(query_bias, "fsdp", axis=0, tiled=True),
        lax.all_gather(value_bias, "fsdp", axis=0, tiled=True),
        lax.all_gather(out_bias, "fsdp", axis=0, tiled=True),
        lax.all_gather(norm_one_gain, "fsdp", axis=0, tiled=True),
        lax.all_gather(norm_one_bias, "fsdp", axis=0, tiled=True),
        lax.all_gather(w_inner, "fsdp", axis=0, tiled=True),
        lax.all_gather(inner_bias, "fsdp", axis=0, tiled=True),
        lax.all_gather(w_outer, "fsdp", axis=0, tiled=True),
        lax.all_gather(outer_bias, "fsdp", axis=0, tiled=True),
        lax.all_gather(norm_two_gain, "fsdp", axis=0, tiled=True),
        lax.all_gather(norm_two_bias, "fsdp", axis=0, tiled=True),
    )
    seqs = doc_ids.shape[0]
    seg = doc_ids.shape[1]
    width = tokens.shape[1]
    mem = read_memory.shape[0] // seqs
    length = seg + 2 * mem
    block = min(512, length)
    factor = HEAD_DIM ** (-0.5)
    memory_rows = read_memory.reshape(seqs, mem, width)
    rows = jnp.concatenate([memory_rows, tokens.reshape(seqs, seg, width), memory_rows], axis=1)
    rows = rows.reshape(seqs * length, width)
    marks = jnp.full((seqs, mem), -1, jnp.int32)
    ids = jnp.concatenate([marks, doc_ids, marks], axis=1)

    def split(value):
        return value.reshape(seqs, length, HEADS, HEAD_DIM)

    query = (product(rows, query_mat) + query_shift.astype(jnp.float32)).astype(jnp.bfloat16)
    keys = product(rows, key_mat).astype(jnp.bfloat16)
    values = (product(rows, value_mat) + value_shift.astype(jnp.float32)).astype(jnp.bfloat16)
    attended, log_sums = lax.map(
        lambda item: attend_forward(item[0], item[1], item[2], item[3], factor, block),
        (split(query), split(keys), split(values), ids),
    )
    attended_low = attended.reshape(seqs * length, width).astype(jnp.bfloat16)
    residual = (
        rows.astype(jnp.float32) + product(attended_low, out_mat) + out_shift.astype(jnp.float32)
    )
    normed, norm_one_pull = jax.vjp(
        layer_norm, residual, gain_one.astype(jnp.float32), shift_one.astype(jnp.float32)
    )
    normed_low = normed.astype(jnp.bfloat16)
    inner = product(normed_low, inner_mat) + inner_shift.astype(jnp.float32)
    active, gelu_pull = jax.vjp(partial(jax.nn.gelu, approximate=False), inner)
    active_low = active.astype(jnp.bfloat16)
    second = normed + product(active_low, outer_mat) + outer_shift.astype(jnp.float32)
    output, norm_two_pull = jax.vjp(
        layer_norm, second, gain_two.astype(jnp.float32), shift_two.astype(jnp.float32)
    )
    back_query, back_key, back_value, back_out, back_inner, back_outer = (
        lax.all_gather(w_query, "fsdp", axis=0, tiled=True),
        lax.all_gather(w_key, "fsdp", axis=0, tiled=True),
        lax.all_gather(w_value, "fsdp", axis=0, tiled=True),
        lax.all_gather(w_out, "fsdp", axis=0, tiled=True),
        lax.all_gather(w_inner, "fsdp", axis=0, tiled=True),
        lax.all_gather(w_outer, "fsdp", axis=0, tiled=True),
    )
    grad_second, grad_gain_two, grad_shift_two = norm_two_pull(out_grad.astype(jnp.float32))
    grad_outer_low = grad_second.astype(jnp.bfloat16)
    grad_w_outer = inner_rows(active_low, grad_outer_low)
    grad_outer_bias = column_sum(grad_outer_low)
    (grad_inner,) = gelu_pull(against(grad_outer_low, back_outer))
    grad_inner_low = grad_inner.astype(jnp.bfloat16)
    grad_w_inner = inner_rows(normed_low, grad_inner_low)
    grad_inner_bias = column_sum(grad_inner_low)
    grad_normed = grad_second + against(grad_inner_low, back_inner)
    grad_residual, grad_gain_one, grad_shift_one = norm_one_pull(grad_normed)
    grad_branch_low = grad_residual.astype(jnp.bfloat16)
    grad_w_out = inner_rows(attended_low, grad_branch_low)
    grad_out_bias = column_sum(grad_branch_low)
    grad_attended = against(grad_branch_low, back_out).astype(jnp.bfloat16)
    grad_query, grad_keys, grad_values = lax.map(
        lambda item: attend_backward(
            item[0], item[1], item[2], item[3], item[4], item[5], factor, block
        ),
        (split(query), split(keys), split(values), ids, log_sums, split(grad_attended)),
    )
    grad_query_low = grad_query.reshape(seqs * length, width).astype(jnp.bfloat16)
    grad_keys_low = grad_keys.reshape(seqs * length, width).astype(jnp.bfloat16)
    grad_values_low = grad_values.reshape(seqs * length, width).astype(jnp.bfloat16)
    grad_w_query = inner_rows(rows, grad_query_low)
    grad_w_key = inner_rows(rows, grad_keys_low)
    grad_w_value = inner_rows(rows, grad_values_low)
    grad_query_bias = column_sum(grad_query_low)
    grad_value_bias = column_sum(grad_values_low)
    grad_rows = (
        grad_residual
        + against(grad_query_low, back_query)
        + against(grad_keys_low, back_key)
        + against(grad_values_low, back_value)
    ).reshape(seqs, length, width)
    grad_tokens = grad_rows[:, mem : mem + seg].reshape(seqs * seg, width).astype(jnp.bfloat16)
    grad_memory = (
        (grad_rows[:, :mem] + grad_rows[:, mem + seg :])
        .reshape(seqs * mem, width)
        .astype(jnp.bfloat16)
    )
    (
        share_wq,
        share_wk,
        share_wv,
        share_wo,
        share_bq,
        share_bv,
        share_bo,
        share_g1,
        share_n1,
        share_w1,
        share_b1,
        share_w2,
        share_b2,
        share_g2,
        share_n2,
    ) = (
        lax.psum_scatter(
            grad_w_query.astype(jnp.bfloat16), "fsdp", scatter_dimension=0, tiled=True
        ).astype(jnp.float32),
        lax.psum_scatter(
            grad_w_key.astype(jnp.bfloat16), "fsdp", scatter_dimension=0, tiled=True
        ).astype(jnp.float32),
        lax.psum_scatter(
            grad_w_value.astype(jnp.bfloat16), "fsdp", scatter_dimension=0, tiled=True
        ).astype(jnp.float32),
        lax.psum_scatter(
            grad_w_out.astype(jnp.bfloat16), "fsdp", scatter_dimension=0, tiled=True
        ).astype(jnp.float32),
        lax.psum_scatter(
            grad_query_bias.astype(jnp.bfloat16), "fsdp", scatter_dimension=0, tiled=True
        ).astype(jnp.float32),
        lax.psum_scatter(
            grad_value_bias.astype(jnp.bfloat16), "fsdp", scatter_dimension=0, tiled=True
        ).astype(jnp.float32),
        lax.psum_scatter(
            grad_out_bias.astype(jnp.bfloat16), "fsdp", scatter_dimension=0, tiled=True
        ).astype(jnp.float32),
        lax.psum_scatter(
            grad_gain_one.astype(jnp.bfloat16), "fsdp", scatter_dimension=0, tiled=True
        ).astype(jnp.float32),
        lax.psum_scatter(
            grad_shift_one.astype(jnp.bfloat16), "fsdp", scatter_dimension=0, tiled=True
        ).astype(jnp.float32),
        lax.psum_scatter(
            grad_w_inner.astype(jnp.bfloat16), "fsdp", scatter_dimension=0, tiled=True
        ).astype(jnp.float32),
        lax.psum_scatter(
            grad_inner_bias.astype(jnp.bfloat16), "fsdp", scatter_dimension=0, tiled=True
        ).astype(jnp.float32),
        lax.psum_scatter(
            grad_w_outer.astype(jnp.bfloat16), "fsdp", scatter_dimension=0, tiled=True
        ).astype(jnp.float32),
        lax.psum_scatter(
            grad_outer_bias.astype(jnp.bfloat16), "fsdp", scatter_dimension=0, tiled=True
        ).astype(jnp.float32),
        lax.psum_scatter(
            grad_gain_two.astype(jnp.bfloat16), "fsdp", scatter_dimension=0, tiled=True
        ).astype(jnp.float32),
        lax.psum_scatter(
            grad_shift_two.astype(jnp.bfloat16), "fsdp", scatter_dimension=0, tiled=True
        ).astype(jnp.float32),
    )
    (
        final_wq,
        final_wk,
        final_wv,
        final_wo,
        final_bq,
        final_bv,
        final_bo,
        final_g1,
        final_n1,
        final_w1,
        final_b1,
        final_w2,
        final_b2,
        final_g2,
        final_n2,
    ) = (
        lax.psum(share_wq.astype(jnp.bfloat16), "rep").astype(jnp.float32),
        lax.psum(share_wk.astype(jnp.bfloat16), "rep").astype(jnp.float32),
        lax.psum(share_wv.astype(jnp.bfloat16), "rep").astype(jnp.float32),
        lax.psum(share_wo.astype(jnp.bfloat16), "rep").astype(jnp.float32),
        lax.psum(share_bq.astype(jnp.bfloat16), "rep").astype(jnp.float32),
        lax.psum(share_bv.astype(jnp.bfloat16), "rep").astype(jnp.float32),
        lax.psum(share_bo.astype(jnp.bfloat16), "rep").astype(jnp.float32),
        lax.psum(share_g1.astype(jnp.bfloat16), "rep").astype(jnp.float32),
        lax.psum(share_n1.astype(jnp.bfloat16), "rep").astype(jnp.float32),
        lax.psum(share_w1.astype(jnp.bfloat16), "rep").astype(jnp.float32),
        lax.psum(share_b1.astype(jnp.bfloat16), "rep").astype(jnp.float32),
        lax.psum(share_w2.astype(jnp.bfloat16), "rep").astype(jnp.float32),
        lax.psum(share_b2.astype(jnp.bfloat16), "rep").astype(jnp.float32),
        lax.psum(share_g2.astype(jnp.bfloat16), "rep").astype(jnp.float32),
        lax.psum(share_n2.astype(jnp.bfloat16), "rep").astype(jnp.float32),
    )
    return (
        output.astype(jnp.bfloat16),
        grad_tokens,
        grad_memory,
        final_wq,
        final_wk,
        final_wv,
        final_wo,
        final_bq,
        final_bv,
        final_bo,
        final_g1,
        final_n1,
        final_w1,
        final_b1,
        final_w2,
        final_b2,
        final_g2,
        final_n2,
    )


def solution(mesh):
    return jax.shard_map(
        on_device,
        mesh=mesh,
        in_specs=(
            P(("rep", "fsdp"), None),
            P(("rep", "fsdp"), None),
            P(("rep", "fsdp"), None),
            P("fsdp", None),
            P("fsdp", None),
            P("fsdp", None),
            P("fsdp", None),
            P("fsdp"),
            P("fsdp"),
            P("fsdp"),
            P("fsdp"),
            P("fsdp"),
            P("fsdp", None),
            P("fsdp"),
            P("fsdp", None),
            P("fsdp"),
            P("fsdp"),
            P("fsdp"),
            P(("rep", "fsdp"), None),
        ),
        out_specs=(
            P(("rep", "fsdp"), None),
            P(("rep", "fsdp"), None),
            P(("rep", "fsdp"), None),
            P("fsdp", None),
            P("fsdp", None),
            P("fsdp", None),
            P("fsdp", None),
            P("fsdp"),
            P("fsdp"),
            P("fsdp"),
            P("fsdp"),
            P("fsdp"),
            P("fsdp", None),
            P("fsdp"),
            P("fsdp", None),
            P("fsdp"),
            P("fsdp"),
            P("fsdp"),
        ),
        check_vma=False,
    )
```

profile of v0, /device:TPU:1, one launch (start us, length us, event | category | flops | bytes accessed | tf_op | source)
XLA Modules:
  0.0 925.9 jit_solution(10924948326763895835)
XLA Ops:
  11.9 1.3 fusion.63
  19.7 31.4 %all-reduce.20 = (bf16[768]{0:T(1024)(128)(2,1)S(1)}, bf16[768]{0:T(1024)(128)(2,1)S(1)}, bf16[768]{0:T(1024)(128)(2,1)S(1)}, bf16[768]{0:T(1024)(128)(2,1)S(1)}...) all-reduce(bf16[768]{0:T(1024)(128)(2,1)S(1)} %dynamic-update-slice, ...), channel_id=1, replica_groups=mesh['rep'=4,'fsdp'=8] {'fsdp'}, use_global_device_ids=true, to_apply=%add.2 | all-reduce | flops 5376 | bytes 21504
  54.0 22.1 %all-gather = bf16[8,1,384]{2,1,0:T(2,128)(2,1)S(1)} all-gather(bf16[1,1,384]{2,1,0:T(2,128)(2,1)S(1)} %reshape.363), channel_id=1, replica_groups=mesh['rep'=4,'fsdp'=8] {'fsdp'}, dimensions={0}, use_global_device_ids=true | all-gather | bytes 6912 | tf_op jit(solution)/shard_map/all_gather | solution.py:147
  78.0 3.6 add_convert_fusion.3
  82.5 11.8 %all-gather.12.cloned.1.call-done = bf16[768,768]{1,0:T(8,128)(2,1)} async-done(((bf16[96,768]{1,0:T(8,128)(2,1)}), bf16[768,768]{1,0:T(8,128)(2,1)}) %all-gather.12.cloned.1.call-update) | async-done | bytes 1179664 | tf_op jit(solution)/shard_map/all_gather | solution.py:138
  94.3 3.2 convolution_convert_fusion.3
  97.6 10.8 %fusion.18 = (f32[12,512]{1,0:T(8,128)S(1)}, f32[12,512,1024]{2,1,0:T(8,128)}) fusion(pred[512,1024]{1,0:T(8,128)(4,1)S(1)} %get-tuple-element.122, bf16[512,12,64]{0,2,1:T(8,128)(2,1)S(1)} %bitcast.103, bf16[1024,12,64]{0,2,1:T(8,128)(2,1)S(1)} %bitcast.97), kind=kOutput, calls=%fused_computation.39 | convolution fusion | flops 824174592 | bytes 28073984 | tf_op jit(solution)/shard_map/while/body/eval_jaxpr/qhd,khd->hqk/dot_general | solution.py:41
  108.4 11.8 %fusion = f32[12,512]{1,0:T(8,128)S(1)} fusion(f32[12,512]{1,0:T(8,128)S(1)} %get-tuple-element.130, f32[12,512,1024]{2,1,0:T(8,128)} %get-tuple-element.131, pred[512,1024]{1,0:T(8,128)(4,1)S(1)} %get-tuple-element.122), kind=kLoop, calls=%fused_computation.12 | loop fusion | flops 25159680 | bytes 25739264 | tf_op jit(solution)/shard_map/while/body/eval_jaxpr/reduce_sum | solution.py:58
  120.8 15.6 %all-gather.8.cloned.1.call-done = bf16[768,768]{1,0:T(8,128)(2,1)} async-done(((bf16[96,768]{1,0:T(8,128)(2,1)}), bf16[768,768]{1,0:T(8,128)(2,1)}) %all-gather.8.cloned.1.call-update) | async-done | bytes 1179664 | tf_op jit(solution)/shard_map/all_gather | solution.py:139
  136.4 3.2 add_convert_fusion.4
  139.6 13.3 %fusion.37 = bf16[512,12,64]{0,2,1:T(8,128)(2,1)} fusion(bf16[1024,12,64]{0,2,1:T(8,128)(2,1)S(1)} %bitcast.105, f32[12,512]{1,0:T(8,128)S(1)} %fusion, f32[12,512]{1,0:T(8,128)S(1)} %get-tuple-element.130, f32[12,512,1024]{2,1,0:T(8,128)} %get-tuple-element.131, pred[512,1024]{1,0:T(8,128)(4,1)S(1)} %get-tuple-element.122), kind=kOutput, calls=%fused_computation.90 | convolution fusion | flops 837156864 | bytes 28098560 | tf_op jit(solution)/shard_map/while/body/eval_jaxpr/hqk,khd->qhd/dot_general | solution.py:60
  152.9 11.1 %fusion.19 = (f32[12,512]{1,0:T(8,128)S(1)}, f32[12,512,1024]{2,1,0:T(8,128)}) fusion(pred[512,1024]{1,0:T(8,128)(4,1)S(1)} %get-tuple-element.123, bf16[512,12,64]{0,2,1:T(8,128)(2,1)S(1)} %bitcast.101, bf16[1024,12,64]{0,2,1:T(8,128)(2,1)S(1)} %bitcast.98), kind=kOutput, calls=%fused_computation.40 | convolution fusion | flops 824174592 | bytes 28073984 | tf_op jit(solution)/shard_map/while/body/eval_jaxpr/qhd,khd->hqk/dot_general | solution.py:41
  164.0 12.3 %fusion.1 = f32[12,512]{1,0:T(8,128)S(1)} fusion(f32[12,512]{1,0:T(8,128)S(1)} %get-tuple-element.128, f32[12,512,1024]{2,1,0:T(8,128)} %get-tuple-element.129, pred[512,1024]{1,0:T(8,128)(4,1)S(1)} %get-tuple-element.123), kind=kLoop, calls=%fused_computation.13 | loop fusion | flops 25159680 | bytes 25739264 | tf_op jit(solution)/shard_map/while/body/eval_jaxpr/reduce_sum | solution.py:58
  177.0 2.5 copy-done
  179.5 7.8 fusion.38
  187.4 1.3 pad_maximum_fusion
  188.7 4.2 fusion.64
  193.4 64.6 %all-gather.16.cloned.1.call-done = bf16[768,3072]{1,0:T(8,128)(2,1)} async-done(((bf16[96,3072]{1,0:T(8,128)(2,1)}), bf16[768,3072]{1,0:T(8,128)(2,1)}) %all-gather.16.cloned.1.call-update) | async-done | bytes 4718608 | tf_op jit(solution)/shard_map/all_gather | solution.py:146
  258.1 35.8 %multiply_convert_fusion.2 = (bf16[1024,3072]{1,0:T(8,128)(2,1)}, f32[1024,3072]{1,0:T(8,128)}, f32[1024,3072]{1,0:T(8,128)}) fusion(f32[3072]{0:T(1024)S(1)} %bitcast.128, bf16[768,3072]{1,0:T(8,128)(2,1)} %all-gather.16.cloned.1.call-done, f32[1024,768]{1,0:T(8,128)S(1)} %get-tuple-element.133, f32[768]{0:T(1024)S(1)} %convert_element_type.257, ...), kind=kOutput, calls=%fused_computation.23 | convolution fusion | flops 5043388416 | bytes 39348224 | tf_op jit(solution)/shard_map/dot_general | solution.py:20
  293.8 44.0 %all-gather.18.cloned.1.call-done = bf16[3072,768]{1,0:T(8,128)(2,1)} async-done(((bf16[384,768]{1,0:T(8,128)(2,1)}), bf16[3072,768]{1,0:T(8,128)(2,1)}) %all-gather.18.cloned.1.call-update) | async-done | bytes 4718608 | tf_op jit(solution)/shard_map/all_gather | solution.py:148
  337.8 9.0 fusion.65
  347.4 2.0 copy-done.7
  349.4 1.8 fusion.23
  351.2 1.5 fusion.59
  352.7 2.1 fusion.55
  354.8 18.7 %fusion.66 = (bf16[3072]{0:T(1024)(128)(2,1)}, bf16[1024,3072]{1,0:T(8,128)(2,1)}) fusion(f32[1024,3072]{1,0:T(8,128)} %get-tuple-element.117, bf16[1024,768]{1,0:T(8,128)(2,1)} %get-tuple-element.107, bf16[3072,768]{1,0:T(8,128)(2,1)} %all-gather.18.cloned.1.call-done, f32[1024,3072]{1,0:T(8,128)} %get-tuple-element.134, f32[3072]{0:T(1024)S(1)} %bitcast.129), kind=kOutput, calls=%fused_computation.133 | convolution fusion | flops 4882166784 | bytes 37767168 | tf_op jit(solution)/shard_map/dot_general | solution.py:30
  373.5 10.1 %multiply_reduce_fusion.2 = (bf16[768]{0:T(1024)(128)(2,1)}, f32[1024]{0:T(1024)S(1)}, bf16[768]{0:T(1024)(128)(2,1)}, f32[1024,768]{1,0:T(8,128)S(1)}) fusion(f32[1024,768]{1,0:T(8,128)S(1)} %get-tuple-element.133, f32[1024]{0:T(1024)S(1)} %fusion.41, f32[1024]{0:T(1024)S(1)} %broadcast_multiply_fusion.1, f32[768]{0:T(1024)S(1)} %convert_element_type.256, ...), kind=kOutput, calls=%fused_computation.52 | convolution fusion | flops 4839699456 | bytes 20469760 | tf_op jit(solution)/shard_map/dot_general | solution.py:30
  383.6 1.5 fusion.58
  385.1 1.7 copy-done.4
  387.8 2.4 convolution_convert_fusion.4
  390.3 1.4 convolution_convert_fusion.2
  392.8 13.8 %fusion.5 = f32[12,64,1024]{2,1,0:T(8,128)} fusion(bf16[512,12,64]{0,2,1:T(8,128)(2,1)S(1)} %bitcast.113, f32[12,512]{1,0:T(8,128)S(1)} %copy-done.31, f32[12,512,1024]{2,1,0:T(8,128)} %get-tuple-element.129, pred[512,1024]{1,0:T(8,128)(4,1)S(1)} %copy-done.12), kind=kOutput, calls=%fused_computation.18 | convolution fusion | flops 830472192 | bytes 29646848 | tf_op jit(solution)/shard_map/while/body/eval_jaxpr/hqk,qhd->khd/dot_general | solution.py:74
  406.7 17.8 %multiply_reduce_fusion.1 = (f32[12,512]{1,0:T(8,128)S(1)}, f32[12,512,1024]{2,1,0:T(8,128)}) fusion(f32[12,512]{1,0:T(8,128)S(1)} %copy-done.30, f32[12,512,1024]{2,1,0:T(8,128)} %get-tuple-element.131, pred[512,1024]{1,0:T(8,128)(4,1)S(1)} %copy-done.10, bf16[512,12,64]{0,2,1:T(8,128)(2,1)} %bitcast.115, bf16[1024,12,64]{0,2,1:T(8,128)(2,1)S(1)} %bitcast.107), kind=kOutput, calls=%fused_computation.4 | convolution fusion | flops 836757504 | bytes 53264384 | tf_op jit(solution)/shard_map/while/body/eval_jaxpr/qhd,khd->hqk/dot_general | solution.py:80
  424.5 13.7 %bitcast_reduce_fusion = (bf16[12,64]{1,0:T(8,128)(2,1)}, bf16[12,64,1024]{2,1,0:T(8,128)(2,1)S(1)}) fusion(f32[12,64,1024]{2,1,0:T(8,128)} %fusion.5, bf16[512,12,64]{0,2,1:T(8,128)(2,1)} %bitcast.116, f32[12,512]{1,0:T(8,128)S(1)} %copy-done.30, f32[12,512,1024]{2,1,0:T(8,128)} %get-tuple-element.131, pred[512,1024]{1,0:T(8,128)(4,1)S(1)} %copy-done.10), kind=kOutput, calls=%fused_computation.80 | convolution fusion | flops 832830720 | bytes 31221248 | tf_op jit(solution)/shard_map/while/body/eval_jaxpr/hqk,qhd->khd/dot_general | solution.py:74
  439.3 2.5 convolution_convert_fusion.5
  441.8 21.6 %multiply_reduce_fusion = (f32[12,512]{1,0:T(8,128)S(1)}, f32[12,512,1024]{2,1,0:T(8,128)}) fusion(f32[12,512]{1,0:T(8,128)S(1)} %copy-done.31, f32[12,512,1024]{2,1,0:T(8,128)} %get-tuple-element.129, pred[512,1024]{1,0:T(8,128)(4,1)S(1)} %copy-done.12, bf16[512,12,64]{0,2,1:T(8,128)(2,1)S(1)} %bitcast.114, bf16[1024,12,64]{0,2,1:T(8,128)(2,1)S(1)} %bitcast.108), kind=kOutput, calls=%fused_computation.1 | convolution fusion | flops 836757504 | bytes 53264384 | tf_op jit(solution)/shard_map/while/body/eval_jaxpr/qhd,khd->hqk/dot_general | solution.py:80
  463.5 42.2 %multiply_convert_fusion = (bf16[12,512,1024]{2,1,0:T(8,128)(2,1)}, bf16[12,512,1024]{2,1,0:T(8,128)(2,1)}) fusion(f32[12,512,1024]{2,1,0:T(8,128)} %get-tuple-element.139, f32[12,512]{1,0:T(8,128)S(1)} %get-tuple-element.138, f32[12,512]{1,0:T(8,128)S(1)} %copy-done.31, f32[12,512,1024]{2,1,0:T(8,128)} %get-tuple-element.129, ...), kind=kLoop, calls=%fused_computation | loop fusion | flops 75497472 | bytes 126976000 | tf_op jit(solution)/shard_map/while/body/eval_jaxpr/convert_element_type | solution.py:84
  505.7 10.0 %multiply_bitcast_fusion = bf16[512,12,64]{0,2,1:T(8,128)(2,1)} fusion(bf16[1024,12,64]{0,2,1:T(8,128)(2,1)} %bitcast.99, bf16[12,512,1024]{2,1,0:T(8,128)(2,1)} %get-tuple-element.146), kind=kOutput, calls=%fused_computation.81 | convolution fusion | flops 806092800 | bytes 14942208 | tf_op jit(solution)/shard_map/while/body/eval_jaxpr/hqk,khd->qhd/dot_general | solution.py:86
  515.7 6.2 multiply_bitcast_fusion.1
  521.9 4.4 fusion.32
  526.6 6.9 fusion.68
  533.5 7.0 multiply_convert_fusion.3
  541.7 2.5 convolution_convert_fusion.6
  544.3 9.9 %convolution_convert_fusion.1 = bf16[768,3072]{1,0:T(8,128)(2,1)} fusion(bf16[1024,3072]{1,0:T(8,128)(2,1)} %get-tuple-element.145, f32[1024,768]{1,0:T(8,128)S(1)} %copy-done.14, f32[768]{0:T(1024)S(1)} %copy-done.43, f32[768]{0:T(1024)S(1)} %convert_element_type.256, f32[1024]{0:T(1024)S(1)} %fusion.41, f32[1024]{0:T(1024)S(1)} %broadcast_multiply_fusion.1), kind=kOutput, calls=%fused_computation.42 | convolution fusion | flops 4838129664 | bytes 14170112 | tf_op jit(solution)/shard_map/dot_general | solution.py:24
  554.3 1.3 copy-done.25
  555.6 9.8 %convolution_convert_fusion = bf16[3072,768]{1,0:T(8,128)(2,1)} fusion(bf16[1024,3072]{1,0:T(8,128)(2,1)} %get-tuple-element.116, bf16[1024,768]{1,0:T(8,128)(2,1)S(1)} %copy-done.25), kind=kOutput, calls=%fused_computation.41 | convolution fusion | flops 4834197504 | bytes 12582912 | tf_op jit(solution)/shard_map/dot_general | solution.py:24
  567.8 1.7 fusion.57
  569.6 28.9 %all-reduce.19 = (bf16[768]{0:T(1024)(128)(2,1)S(1)}, bf16[768]{0:T(1024)(128)(2,1)S(1)}, bf16[768]{0:T(1024)(128)(2,1)S(1)}, bf16[768]{0:T(1024)(128)(2,1)S(1)}...) all-reduce(bf16[768]{0:T(1024)(128)(2,1)S(1)} %dynamic-update-slice, ...), channel_id=1, replica_groups=mesh['rep'=4,'fsdp'=8] {'fsdp'}, use_global_device_ids=true, to_apply=%add.9 | all-reduce | flops 9984 | bytes 39936
  599.1 13.4 %all-reduce.21 = (bf16[96]{0:T(256)(128)(2,1)S(1)}, bf16[96]{0:T(256)(128)(2,1)S(1)}, bf16[96]{0:T(256)(128)(2,1)S(1)}, bf16[96]{0:T(256)(128)(2,1)S(1)}, bf16[9...) all-reduce(bf16[96]{0:T(256)(128)(2,1)S(1)} %dynamic-slice.10, ...), channel_id=1, replica_groups=mesh['rep'=4,'fsdp'=8] {'rep'}, use_global_device_ids=true, to_apply=%region_24.25 | all-reduce | flops 1152 | bytes 4608 | tf_op jit(solution)/shard_map/psum | solution.py:323
  617.3 2.8 fusion.69
  620.1 1.5 fusion.67
  622.8 3.6 add_bitcast_fusion
  626.5 35.2 %reduce-scatter.9.cloned.1.call-done = bf16[96,768]{1,0:T(8,128)(2,1)} async-done(((bf16[768,768]{1,0:T(8,128)(2,1)}), bf16[96,768]{1,0:T(8,128)(2,1)}) %reduce-scatter.9.cloned.1.call-update) | async-done | bytes 147472 | tf_op jit(solution)/shard_map/reduce_scatter | solution.py:259
  661.7 99.9 %reduce-scatter.15.cloned.1.call-done = bf16[96,3072]{1,0:T(8,128)(2,1)} async-done(((bf16[768,3072]{1,0:T(8,128)(2,1)}), bf16[96,3072]{1,0:T(8,128)(2,1)}) %reduce-scatter.15.cloned.1.call-update) | async-done | bytes 589840 | tf_op jit(solution)/shard_map/reduce_scatter | solution.py:283
  761.6 98.8 %reduce-scatter.17.cloned.1.call-done = bf16[384,768]{1,0:T(8,128)(2,1)} async-done(((bf16[3072,768]{1,0:T(8,128)(2,1)}), bf16[384,768]{1,0:T(8,128)(2,1)}) %reduce-scatter.17.cloned.1.call-update) | async-done | bytes 589840 | tf_op jit(solution)/shard_map/reduce_scatter | solution.py:289
  860.4 1.4 fusion.40
  861.9 3.3 fusion.31
  865.2 1.7 add_convert_fusion.2
  866.9 42.3 %all-reduce.25.cloned.1.call-done = (bf16[96,768]{1,0:T(8,128)(2,1)}, bf16[96,768]{1,0:T(8,128)(2,1)}, bf16[96,768]{1,0:T(8,128)(2,1)}, bf16[96,768]{1,0:T(8,128...) async-done(((bf16[96,768]{1,0:T(8,128)(2,1)}, bf16[96,768]{1,0:T(8,128)(2,1)}, bf16[96,768]{1,0:T(8,128)(2,1)}, bf16[96,768]{1,0:T(8,128)(2,1)}, ...) | async-done | bytes 1769488 | tf_op jit(solution)/shard_map/psum | solution.py:319
  909.2 1.7 convert_element_type.286
  910.9 1.6 convert_element_type.288
  912.5 1.6 convert_element_type.290
  914.2 1.6 convert_element_type.292
  915.8 2.2 convert_element_type.301
  (210 shorter events, 31.9 us)
Async XLA Ops:
  7.2 70.8 %all-gather.10.cloned.1.call-start = ((), (), s32[]{:S(2)}) async-start(), calls=%async_computation.7 | async-start | bytes 1327104 | tf_op jit(solution)/shard_map/all_gather | solution.py:137
  7.9 86.4 %all-gather.12.cloned.1.call-start = ((), (), s32[]{:S(2)}) async-start(), calls=%async_computation.8 | async-start | bytes 1327104 | tf_op jit(solution)/shard_map/all_gather | solution.py:138
  8.7 127.7 %all-gather.8.cloned.1.call-start = ((), (), s32[]{:S(2)}) async-start(), calls=%async_computation.6 | async-start | bytes 1327104 | tf_op jit(solution)/shard_map/all_gather | solution.py:139
  9.4 179.3 %all-gather.14.cloned.1.call-start = ((), (), s32[]{:S(2)}) async-start(), calls=%async_computation.9 | async-start | bytes 1327104 | tf_op jit(solution)/shard_map/all_gather | solution.py:140
  10.0 248.1 %all-gather.16.cloned.1.call-start = ((), (), s32[]{:S(2)}) async-start(), calls=%async_computation.10 | async-start | bytes 5308416 | tf_op jit(solution)/shard_map/all_gather | solution.py:146
  10.6 327.3 %all-gather.18.cloned.1.call-start = ((), (), s32[]{:S(2)}) async-start(), calls=%async_computation.11 | async-start | bytes 5308416 | tf_op jit(solution)/shard_map/all_gather | solution.py:148
  11.1 615.3 %reduce-scatter.13.cloned.1.call-start = ((), (), s32[]{:S(2)}) async-start(), calls=%async_computation.15 | async-start | bytes 1327104 | tf_op jit(solution)/shard_map/reduce_scatter | solution.py:265
  52.7 285.1 %copy-start.42 = (f32[768]{0:T(1024)}, f32[768]{0:T(1024)S(1)}, u32[]{:S(2)}) copy-start(f32[768]{0:T(1024)S(1)} %convert_element_type.257) | copy-start | bytes 9220
  77.9 61.7 %copy-start.9 = (pred[512,1024]{1,0:T(8,128)(4,1)}, pred[512,1024]{1,0:T(8,128)(4,1)S(1)}, u32[]{:S(2)}) copy-start(pred[512,1024]{1,0:T(8,128)(4,1)S(1)} %get-tuple-element.122) | copy-start | bytes 1572868
  77.9 99.1 %copy-start.11 = (pred[512,1024]{1,0:T(8,128)(4,1)}, pred[512,1024]{1,0:T(8,128)(4,1)S(1)}, u32[]{:S(2)}) copy-start(pred[512,1024]{1,0:T(8,128)(4,1)S(1)} %get-tuple-element.123) | copy-start | bytes 1572868
  78.0 16.4 %copy-start.52 = (bf16[10,768]{1,0:T(8,128)(2,1)S(1)}, bf16[10,768]{1,0:T(8,128)(2,1)}, u32[]{:S(2)}) copy-start(bf16[10,768]{1,0:T(8,128)(2,1)} %param.20) | copy-start | bytes 46084
  82.5 70.4 %copy-start.15 = (bf16[512,768]{0,1:T(8,128)(2,1)}, bf16[512,768]{0,1:T(8,128)(2,1)S(1)}, u32[]{:S(2)}) copy-start(bf16[512,768]{0,1:T(8,128)(2,1)S(1)} %get-tuple-element.121) | copy-start | bytes 2359300
  94.3 3.3 copy-start.17
  97.6 55.3 %copy-start.6 = (bf16[1024,768]{0,1:T(8,128)(2,1)}, bf16[1024,768]{0,1:T(8,128)(2,1)S(1)}, u32[]{:S(2)}) copy-start(bf16[1024,768]{0,1:T(8,128)(2,1)S(1)} %convolution_convert_fusion.3) | copy-start | bytes 4718596
  139.6 37.5 %copy-start.19 = (bf16[1024,768]{0,1:T(8,128)(2,1)}, bf16[1024,768]{0,1:T(8,128)(2,1)S(1)}, u32[]{:S(2)}) copy-start(bf16[1024,768]{0,1:T(8,128)(2,1)S(1)} %add_convert_fusion.4) | copy-start | bytes 4718596
  164.0 15.5 %copy-start = (f32[12,512,1024]{2,1,0:T(8,128)S(1)}, f32[12,512,1024]{2,1,0:T(8,128)}, u32[]{:S(2)}) copy-start(f32[12,512,1024]{2,1,0:T(8,128)} %get-tuple-element.129) | copy-start | bytes 75497472
  179.5 7.8 copy-start.28
  192.9 190.7 %copy-start.13 = (f32[1024,768]{1,0:T(8,128)}, f32[1024,768]{1,0:T(8,128)S(1)}, u32[]{:S(2)}) copy-start(f32[1024,768]{1,0:T(8,128)S(1)} %get-tuple-element.133) | copy-start | bytes 9437188
  258.1 79.8 %copy-start.45 = (f32[768]{0:T(1024)S(1)}, f32[768]{0:T(1024)}, u32[]{:S(2)}) copy-start(f32[768]{0:T(1024)} %convert_element_type.261) | copy-start | bytes 9220
  346.8 4.4 copy-start.2
  346.8 2.5 copy-start.7
  346.9 2.5 copy-start.34
  346.9 4.3 copy-start.32
  349.4 3.3 copy-start.36
  385.1 1.8 copy-start.4
  385.1 2.7 copy-start.26
  387.8 2.5 copy-start.51
  390.2 236.2 %reduce-scatter.11.cloned.1.call-start = ((), (), s32[]{:S(2)}) async-start(), calls=%async_computation.14 | async-start | bytes 1327104 | tf_op jit(solution)/shard_map/reduce_scatter | solution.py:262
  392.8 13.8 %copy-start.10 = (pred[512,1024]{1,0:T(8,128)(4,1)S(1)}, pred[512,1024]{1,0:T(8,128)(4,1)}, u32[]{:S(2)}) copy-start(pred[512,1024]{1,0:T(8,128)(4,1)} %copy-done.9) | copy-start | bytes 1572868
  392.8 13.8 %copy-start.20 = (bf16[1024,768]{0,1:T(8,128)(2,1)S(1)}, bf16[1024,768]{0,1:T(8,128)(2,1)}, u32[]{:S(2)}) copy-start(bf16[1024,768]{0,1:T(8,128)(2,1)} %copy-done.19) | copy-start | bytes 4718596
  392.8 13.8 %copy-start.30 = (f32[12,512]{1,0:T(8,128)S(1)}, f32[12,512]{1,0:T(8,128)}, u32[]{:S(2)}) copy-start(f32[12,512]{1,0:T(8,128)} %log_add_fusion.1) | copy-start | bytes 73732
  424.5 14.8 %copy-start.48 = (bf16[1004,768]{1,0:T(8,128)(2,1)S(1)}, bf16[1004,768]{1,0:T(8,128)(2,1)}, u32[]{:S(2)}) copy-start(bf16[1004,768]{1,0:T(8,128)(2,1)} %param.19) | copy-start | bytes 4626436
  424.5 14.8 %copy-start.53 = (bf16[10,768]{1,0:T(8,128)(2,1)S(1)}, bf16[10,768]{1,0:T(8,128)(2,1)}, u32[]{:S(2)}) copy-start(bf16[10,768]{1,0:T(8,128)(2,1)} %param.20) | copy-start | bytes 46084
  463.5 163.0 %reduce-scatter.7.cloned.1.call-start = ((), (), s32[]{:S(2)}) async-start(), calls=%async_computation.12 | async-start | bytes 1327104 | tf_op jit(solution)/shard_map/reduce_scatter | solution.py:256
  505.7 10.0 %copy-start.1 = (bf16[12,512,1024]{2,1,0:T(8,128)(2,1)S(1)}, bf16[12,512,1024]{2,1,0:T(8,128)(2,1)}, u32[]{:S(2)}) copy-start(bf16[12,512,1024]{2,1,0:T(8,128)(2,1)} %get-tuple-element.147) | copy-start | bytes 37748740
  515.7 6.2 copy-start.54
  521.9 4.7 copy-start.18
  526.3 7.2 copy-start.16
  526.3 135.3 %reduce-scatter.9.cloned.1.call-start = ((), (), s32[]{:S(2)}) async-start(), calls=%async_computation.13 | async-start | bytes 1327104 | tf_op jit(solution)/shard_map/reduce_scatter | solution.py:259
  533.5 8.2 copy-start.49
  541.7 2.5 copy-start.14
  541.7 2.6 copy-start.43
  544.2 217.4 %reduce-scatter.15.cloned.1.call-start = ((), (), s32[]{:S(2)}) async-start(), calls=%async_computation.16 | async-start | bytes 5308416 | tf_op jit(solution)/shard_map/reduce_scatter | solution.py:283
  554.3 306.2 %reduce-scatter.17.cloned.1.call-start = ((), (), s32[]{:S(2)}) async-start(), calls=%async_computation.17 | async-start | bytes 5308416 | tf_op jit(solution)/shard_map/reduce_scatter | solution.py:289
  565.4 1.7 copy-start.8
  565.5 2.0 copy-start.55
  565.5 2.3 copy-start.44
  565.5 4.1 copy-start.38
  565.5 4.1 copy-start.39
  565.5 4.0 copy-start.40
  565.5 4.0 copy-start.41
  565.5 4.0 copy-start.46
  565.5 4.0 copy-start.47
  565.5 51.7 %copy-start.22 = (bf16[12,64,1024]{2,1,0:T(8,128)(2,1)S(1)}, bf16[12,64,1024]{2,1,0:T(8,128)(2,1)}, u32[]{:S(2)}) copy-start(bf16[12,64,1024]{2,1,0:T(8,128)(2,1)} %copy-done.21) | copy-start | bytes 4718596
  565.6 343.6 %all-reduce.25.cloned.1.call-start = ((), (), s32[]{:S(2)}) async-start(), calls=%async_computation.18 | async-start | bytes 3538944 | tf_op jit(solution)/shard_map/psum | solution.py:319
  617.3 2.8 copy-start.50
  620.1 1.9 copy-start.5
  620.1 2.4 copy-start.24
  620.1 2.7 copy-start.27
  626.4 238.8 %copy-start.3 = (f32[1024,768]{1,0:T(8,128)S(1)}, f32[1024,768]{1,0:T(8,128)}, u32[]{:S(2)}) copy-start(f32[1024,768]{1,0:T(8,128)} %copy-done.2) | copy-start | bytes 9437188
  626.4 238.8 %copy-start.33 = (f32[1024]{0:T(1024)S(1)}, f32[1024]{0:T(1024)}, u32[]{:S(2)}) copy-start(f32[1024]{0:T(1024)} %copy-done.32) | copy-start | bytes 12292
  626.4 238.8 %copy-start.35 = (f32[768]{0:T(1024)S(1)}, f32[768]{0:T(1024)}, u32[]{:S(2)}) copy-start(f32[768]{0:T(1024)} %convert_element_type.262) | copy-start | bytes 9220
  626.4 238.8 %copy-start.37 = (f32[1024]{0:T(1024)S(1)}, f32[1024]{0:T(1024)}, u32[]{:S(2)}) copy-start(f32[1024]{0:T(1024)} %copy-done.36) | copy-start | bytes 12292
  909.2 8.8 copy-start.29
  (5 other events, 5.9 us)
Sparse Core Ops, SparseCore 0:
  10.2 41.9 all-gather.9
  54.4 39.9 all-gather.11
  96.5 39.8 all-gather.7
  138.4 39.6 all-gather.13
  180.2 77.8 all-gather.15
  260.1 77.6 all-gather.17
  390.4 62.7 reduce-scatter.12
  463.6 62.7 reduce-scatter.10
  530.3 63.6 reduce-scatter.6
  597.8 63.8 reduce-scatter.8
  665.3 96.2 reduce-scatter.14
  765.1 95.2 reduce-scatter.16
  863.2 45.9 all-reduce.24
where the time goes:
time: 930 us; the launch traced here: 926 us
  waiting for transfers between devices  416 us (45%)
  matrix products  269 us (29%)
  other arithmetic  101 us (11%)
  blocking collectives  95.8 us (10%)
  local copies, waits for them, and re-layouts  26.4 us (3%)
  between operations  17.1 us (2%)
    reduce_scatter x1, waiting for transfers between devices, on_device(): lax.psum_scatter(grad_w_inner.astype(jnp.bfloat16), 'fsdp', scatter_dimen...  99.9 us
    reduce_scatter x1, waiting for transfers between devices, on_device(): lax.psum_scatter(grad_w_outer.astype(jnp.bfloat16), 'fsdp', scatter_dimen...  98.8 us
    all_gather x1, waiting for transfers between devices, on_device(): lax.all_gather(w_inner, 'fsdp', axis=0, tiled=True)  64.6 us
    unnamed x2, blocking collectives  60.3 us
    dot_general x6, matrix products, product(): return jnp.dot(left, right, preferred_element_type=jnp.float32)  58.9 us
    all_gather x1, waiting for transfers between devices, on_device(): lax.all_gather(w_outer, 'fsdp', axis=0, tiled=True)  44 us
    psum x1, waiting for transfers between devices, on_device(): lax.psum(share_wq.astype(jnp.bfloat16), 'rep').astype(jnp.float32)  42.3 us
    convert_element_type x1, other arithmetic, attend_backward(): grad_scores = (probs * (grad_probs - centre)).astype(jnp.bfloat16)  42.2 us
  transfers between devices with their start and end apart: 13, of which 8 were waited for; matrix products, arithmetic and copies ran while one was open for 35% of the time, Pallas kernels for 0%

commit v1 on v0

--- a/solution.py
+++ b/solution.py
@@ -3,12 +3,416 @@
 import jax
 import jax.numpy as jnp
 from jax import lax
+from jax.experimental import pallas as pl
+from jax.experimental.pallas import tpu as pltpu
 from jax.sharding import PartitionSpec as P
+
+MESH_ID = pl.DeviceIdType.MESH
+W = 768
+
+
+class Copies:
+    def __init__(self, send, recv):
+        self.send, self.recv, self.made = send, recv, {}
+
+    def start(self, name, src, dst, to):
+        slot = len(self.made)
+        copy = pltpu.make_async_remote_copy(
+            src_ref=src,
+            dst_ref=dst,
+            send_sem=self.send.at[slot],
+            recv_sem=self.recv.at[slot],
+            device_id=to,
+            device_id_type=MESH_ID,
+        )
+        copy.start()
+        self.made[name] = copy
+
+    def arrived(self, name):
+        self.made[name].wait_recv()
+
+    def drain(self):
+        for copy in self.made.values():
+            copy.wait_send()
+
+
+def place():
+    rep, owner = lax.axis_index("rep"), lax.axis_index("fsdp")
+    y, c, z, x = rep // 2, rep % 2, owner // 2, owner % 2
+    where = {
+        "core": (y * 2 + 1 - c, owner),
+        "y": ((1 - y) * 2 + c, owner),
+        "x": (rep, z * 2 + 1 - x),
+    }
+    for k in (1, 2, 3):
+        where["z", k] = (rep, ((z + k) % 4) * 2 + x)
+        where["zx", k] = (rep, ((z + k) % 4) * 2 + 1 - x)
+    return rep, owner, y, c, z, x, where
+
+
+def greet(where):
+    barrier = pltpu.get_barrier_semaphore()
+    for to in where.values():
+        pl.semaphore_signal(barrier, inc=1, device_id=to, device_id_type=MESH_ID)
+    pl.semaphore_wait(barrier, len(where))
+
+
+def gather_kernel(a0, a1, a2, av, o0, o1, o2, ov, send, recv, own_sem):
+    rep, owner, y, c, z, x, where = place()
+    part = W // 8
+
+    def in0(k, other_x):
+        z_of, x_of = (z - k + 4) % 4, (1 - x if other_x else x)
+        return o0.at[pl.ds(c * 2, 2), pl.ds((z_of * 2 + x_of) * part, part), :]
+
+    def in1(k, other_x, quarter):
+        z_of, x_of = (z - k + 4) % 4, (1 - x if other_x else x)
+        return o1.at[quarter, pl.ds((z_of * 2 + x_of) * part, part), :]
+
+    def in2(k, other_x, quarter):
+        z_of, x_of = (z - k + 4) % 4, (1 - x if other_x else x)
+        return o2.at[pl.ds((z_of * 2 + x_of) * 4 * part + quarter * part, part), :]
+
+    mine, across = rep, (1 - y) * 2 + c
+    greet(where)
+    own = [
+        pltpu.make_async_copy(a0, o0.at[:, pl.ds(owner * part, part), :], own_sem.at[0]),
+        pltpu.make_async_copy(a2, o2.at[pl.ds(owner * 4 * part, 4 * part), :], own_sem.at[1]),
+        pltpu.make_async_copy(av, ov.at[owner], own_sem.at[2]),
+    ]
+    for r in range(4):
+        own.append(
+            pltpu.make_async_copy(
+                a1.at[:, r * W : (r + 1) * W],
+                o1.at[r, pl.ds(owner * part, part), :],
+                own_sem.at[3 + r],
+            )
+        )
+    copies = Copies(send, recv)
+    from0 = a0.at[pl.ds(c * 2, 2), :, :]
+    from1 = a1.at[:, pl.ds(pl.multiple_of(rep * W, W), W)]
+    from2 = a2.at[pl.ds(rep * part, part), :]
+    for k in (1, 3, 2):
+        copies.start((1, "z", k), from1, in1(0, False, mine), where["z", k])
+        copies.start((2, "z", k), from2, in2(0, False, mine), where["z", k])
+        copies.start((0, "z", k), from0, in0(0, False), where["z", k])
+    copies.start((1, "x", 0), from1, in1(0, False, mine), where["x"])
+    copies.start((2, "x", 0), from2, in2(0, False, mine), where["x"])
+    copies.start((0, "x", 0), from0, in0(0, False), where["x"])
+    for k in (1, 2, 3):
+        copies.start(("v", "z", k), av, ov.at[owner], where["z", k])
+        copies.start(("v", "zx", k), av, ov.at[owner], where["zx", k])
+    copies.start(("v", "x", 0), av, ov.at[owner], where["x"])
+    for copy in own:
+        copy.start()
+
+    def pass_on(k, other_x, stage):
+        for g in (1, 2, 0):
+            copies.arrived((g, stage, k))
+            here = (
+                in0(k, other_x)
+                if g == 0
+                else in1(k, other_x, mine) if g == 1 else in2(k, other_x, mine)
+            )
+            if stage == "z":
+                copies.start((g, "x", k), here, here, where["x"])
+            if g > 0:
+                copies.start((g, "y", k, other_x), here, here, where["y"])
+            copies.start((g, "core", k, other_x), here, here, where["core"])
+
+    order = [(0, True, "x"), (1, False, "z"), (3, False, "z"), (1, True, "x"), (2, False, "z")]
+    order += [(3, True, "x"), (2, True, "x")]
+    for step in order:
+        pass_on(*step)
+    for k, other_x, _ in order:
+        for g in (1, 2):
+            copies.arrived((g, "y", k, other_x))
+            here = in1(k, other_x, across) if g == 1 else in2(k, other_x, across)
+            copies.start((g, "diagonal", k, other_x), here, here, where["core"])
+    for k, other_x, _ in order:
+        for g in (0, 1, 2):
+            copies.arrived((g, "core", k, other_x))
+        for g in (1, 2):
+            copies.arrived((g, "diagonal", k, other_x))
+    for k in (1, 2, 3):
+        copies.arrived(("v", "z", k))
+        copies.arrived(("v", "zx", k))
+    copies.arrived(("v", "x", 0))
+    copies.drain()
+    for copy in own:
+        copy.wait()
+
+
+GATHER_COPIES = 3 * 3 + 3 + 7 + (3 * 3 + 2 * 7 + 3 * 7 + 2 * 7)
+
+
+def gather_all(stack, inner, outer, vectors):
+    low = jnp.bfloat16
+    anywhere = pl.BlockSpec(memory_space=pl.ANY)
+    return pl.pallas_call(
+        gather_kernel,
+        out_shape=(
+            jax.ShapeDtypeStruct((4, W, W), low),
+            jax.ShapeDtypeStruct((4, W, W), low),
+            jax.ShapeDtypeStruct((4 * W, W), low),
+            jax.ShapeDtypeStruct((8,) + vectors.shape, vectors.dtype),
+        ),
+        in_specs=[pl.BlockSpec(memory_space=pltpu.VMEM)] * 4,
+        out_specs=[anywhere] * 4,
+        scratch_shapes=[
+            pltpu.SemaphoreType.DMA((GATHER_COPIES,)),
+            pltpu.SemaphoreType.DMA((GATHER_COPIES,)),
+            pltpu.SemaphoreType.DMA((7,)),
+        ],
+        compiler_params=pltpu.CompilerParams(collective_id=0, has_side_effects=True),
+        name="gather_weights",
+    )(stack, inner, outer, vectors)
+
+
+def total(*refs):
+    value = refs[0][...].astype(jnp.float32)
+    for ref in refs[1:]:
+        value = value + ref[...].astype(jnp.float32)
+    return value
+
+
+def reduce_kernel(
+    g0, g1, g2, gv, r0, r1, r2, rv,
+    k0, c0, x0, z0, e0, k1, c1, y1, x1, z1, e1, got, vec, send, recv, own_sem, out_sem,
+):
+    rep, owner, y, c, z, x, where = place()
+    part = W // 8
+    low = jnp.bfloat16
+    flat = [(k, o) for o in (1, 0) for k in (1, 3, 2, 0)]
+    slot = {pair: i for i, pair in enumerate(flat)}
+
+    def shard(k, o):
+        return ((z + k) % 4) * 2 + (1 - x if o else x)
+
+    def part0(half, k, o):
+        return g0.at[pl.ds(half * 2, 2), pl.ds(shard(k, o) * part, part), :]
+
+    def part1(quarter, k, o):
+        return g1.at[quarter, pl.ds(shard(k, o) * part, part), :]
+
+    def part2(quarter, k, o):
+        return g2.at[pl.ds(shard(k, o) * 4 * part + quarter * part, part), :]
+
+    pieces = {1: part1, 2: part2}
+    greet(where)
+    copies = Copies(send, recv)
+    own = {}
+
+    def load(name, src, dst):
+        copy = pltpu.make_async_copy(src, dst, own_sem.at[len(own)])
+        copy.start()
+        own[name] = copy
+
+    for side in (1, 0):
+        quarter_row = (1 - y) if side else y
+        for pair in flat:
+            i = slot[pair]
+            for g in (1, 2):
+                piece = pieces[g]
+                copies.start(
+                    (g, "core", side, i), piece(quarter_row * 2 + 1 - c, *pair),
+                    c1.at[g - 1, side, i], where["core"],
+                )
+                load((g, side, i), piece(quarter_row * 2 + c, *pair), k1.at[g - 1, side, i])
+            if side:
+                copies.start((0, "core", i), part0(1 - c, *pair), c0.at[i], where["core"])
+                load((0, i), part0(c, *pair), k0.at[i])
+    for k in (1, 2, 3):
+        copies.start(("v", "z", k), gv.at[shard(k, 0)], got.at[k], where["z", k])
+        copies.start(("v", "zx", k), gv.at[shard(k, 1)], got.at[3 + k], where["zx", k])
+    copies.start(("v", "x", 0), gv.at[shard(0, 1)], got.at[7], where["x"])
+
+    def ready(g, *rest):
+        own[(g,) + rest].wait()
+        copies.arrived((g, "core") + rest)
+
+    for pair in flat:
+        i = slot[pair]
+        for g in (1, 2):
+            ready(g, 1, i)
+            k1[g - 1, 1, i] = total(k1.at[g - 1, 1, i], c1.at[g - 1, 1, i]).astype(low)
+            copies.start((g, "y", i), k1.at[g - 1, 1, i], y1.at[g - 1, i], where["y"])
+        if pair[1] == 1:
+            ready(0, i)
+            k0[i] = total(k0.at[i], c0.at[i]).astype(low)
+            copies.start((0, "x", i), k0.at[i], x0.at[i], where["x"])
+    for pair in flat:
+        k, o = pair
+        i = slot[pair]
+        j = slot[k, 1]
+        if o == 1:
+            for g in (1, 2):
+                ready(g, 0, i)
+                copies.arrived((g, "y", i))
+                k1[g - 1, 0, i] = total(
+                    k1.at[g - 1, 0, i], c1.at[g - 1, 0, i], y1.at[g - 1, i]
+                ).astype(low)
+                copies.start((g, "x", i), k1.at[g - 1, 0, i], x1.at[g - 1, i], where["x"])
+        elif k > 0:
+            ready(0, i)
+            copies.arrived((0, "x", j))
+            k0[i] = total(k0.at[i], c0.at[i], x0.at[j]).astype(low)
+            copies.start((0, "z", k), k0.at[i], z0.at[k - 1], where["z", k])
+            for g in (1, 2):
+                ready(g, 0, i)
+                copies.arrived((g, "y", i))
+                copies.arrived((g, "x", j))
+                k1[g - 1, 0, i] = total(
+                    k1.at[g - 1, 0, i], c1.at[g - 1, 0, i], y1.at[g - 1, i], x1.at[g - 1, j]
+                ).astype(low)
+                copies.start((g, "z", k), k1.at[g - 1, 0, i], z1.at[g - 1, k - 1], where["z", k])
+    for k in (1, 2, 3):
+        copies.arrived(("v", "z", k))
+        copies.arrived(("v", "zx", k))
+    copies.arrived(("v", "x", 0))
+    load("v", gv.at[owner], got.at[0])
+    own["v"].wait()
+    value = got[0]
+    for i in range(1, 8):
+        value = value + got[i]
+    vec[0] = value
+    copies.start(("v", "core"), vec.at[0], vec.at[1], where["core"])
+    i, j = slot[0, 0], slot[0, 1]
+    ready(0, i)
+    copies.arrived((0, "x", j))
+    for k in (1, 2, 3):
+        copies.arrived((0, "z", k))
+    e0[0] = total(k0.at[i], c0.at[i], x0.at[j], z0.at[0], z0.at[1], z0.at[2]).astype(low)
+    copies.start((0, "y"), e0.at[0], e0.at[1], where["y"])
+    for g in (1, 2):
+        ready(g, 0, i)
+        copies.arrived((g, "y", i))
+        copies.arrived((g, "x", j))
+        for k in (1, 2, 3):
+            copies.arrived((g, "z", k))
+        e1[g - 1, 0] = total(
+            k1.at[g - 1, 0, i], c1.at[g - 1, 0, i], y1.at[g - 1, i], x1.at[g - 1, j],
+            z1.at[g - 1, 0], z1.at[g - 1, 1], z1.at[g - 1, 2],
+        ).astype(low)
+        copies.start((g, "ey"), e1.at[g - 1, 0], e1.at[g - 1, 1], where["y"])
+        copies.start((g, "ecore"), e1.at[g - 1, 0], e1.at[g - 1, 2], where["core"])
+    copies.arrived(("v", "core"))
+    vec[2] = vec[0] + vec[1]
+    copies.start(("v", "y"), vec.at[2], vec.at[3], where["y"])
+    copies.arrived((0, "y"))
+    e0[2] = total(e0.at[0], e0.at[1]).astype(low)
+    copies.start((0, "ecore"), e0.at[2], e0.at[3], where["core"])
+    for g in (1, 2):
+        copies.arrived((g, "ey"))
+        copies.start((g, "ediagonal"), e1.at[g - 1, 1], e1.at[g - 1, 3], where["core"])
+    r0[pl.ds(c * 2, 2)] = e0[2].astype(jnp.float32)
+    outs = (rep, (1 - y) * 2 + c, y * 2 + 1 - c, (1 - y) * 2 + 1 - c)
+    for g, r in ((1, r1), (2, r2)):
+        r[outs[0]] = e1[g - 1, 0].astype(jnp.float32)
+        r[outs[1]] = e1[g - 1, 1].astype(jnp.float32)
+        copies.arrived((g, "ecore"))
+        r[outs[2]] = e1[g - 1, 2].astype(jnp.float32)
+    copies.arrived(("v", "y"))
+    rv[...] = vec[2] + vec[3]
+    copies.arrived((0, "ecore"))
+    r0[pl.ds((1 - c) * 2, 2)] = e0[3].astype(jnp.float32)
+    for g, r in ((1, r1), (2, r2)):
+        copies.arrived((g, "ediagonal"))
+        r[outs[3]] = e1[g - 1, 3].astype(jnp.float32)
+    copies.drain()
+
+
+REDUCE_COPIES = 2 * 16 + 8 + 7 + 16 + 4 + 8 + 9 + 1 + 1 + 4 + 1 + 1 + 2
+
+
+def reduce_all(stack, inner, outer, vectors):
+    low, full = jnp.bfloat16, jnp.float32
+    part = W // 8
+    anywhere, near = pl.BlockSpec(memory_space=pl.ANY), pl.BlockSpec(memory_space=pltpu.VMEM)
+    return pl.pallas_call(
+        reduce_kernel,
+        out_shape=(
+            jax.ShapeDtypeStruct((4, part, W), full),
+            jax.ShapeDtypeStruct((4, part, W), full),
+            jax.ShapeDtypeStruct((4, part, W), full),
+            jax.ShapeDtypeStruct(vectors.shape[1:], full),
+        ),
+        in_specs=[anywhere] * 4,
+        out_specs=[near] * 4,
+        scratch_shapes=[
+            pltpu.VMEM((8, 2, part, W), low),
+            pltpu.VMEM((8, 2, part, W), low),
+            pltpu.VMEM((4, 2, part, W), low),
+            pltpu.VMEM((3, 2, part, W), low),
+            pltpu.VMEM((4, 2, part, W), low),
+            pltpu.VMEM((2, 2, 8, part, W), low),
+            pltpu.VMEM((2, 2, 8, part, W), low),
+            pltpu.VMEM((2, 8, part, W), low),
+            pltpu.VMEM((2, 4, part, W), low),
+            pltpu.VMEM((2, 3, part, W), low),
+            pltpu.VMEM((2, 4, part, W), low),
+            pltpu.VMEM(vectors.shape, full),
+            pltpu.VMEM((4,) + vectors.shape[1:], full),
+            pltpu.SemaphoreType.DMA((REDUCE_COPIES,)),
+            pltpu.SemaphoreType.DMA((REDUCE_COPIES,)),
+            pltpu.SemaphoreType.DMA((2 * 16 + 8 + 1,)),
+            pltpu.SemaphoreType.DMA((1,)),
+        ],
+        compiler_params=pltpu.CompilerParams(
+            collective_id=1, has_side_effects=True, vmem_limit_bytes=56 << 20
+        ),
+        name="reduce_gradients",
+    )(stack, inner, outer, vectors)
+
+
+SMALL = 9
+
+
+def pack_shard(values, part):
+    flat = jnp.concatenate([value.reshape(-1) for value in values])
+    room = -(-flat.shape[0] // 2048) * 2048
+    return jnp.pad(flat, (0, room - flat.shape[0])).reshape(-1, 128)
+
+
+def unpack_full(packed, part):
+    flat = packed.reshape(packed.shape[0], -1)
+    ends = [part * i for i in range(9)] + [part * 12]
+    return [flat[:, lo:hi].reshape(-1) for lo, hi in zip(ends[:-1], ends[1:])]
+
+
+def pack_full(vectors, owners, part):
+    flat = jnp.concatenate([value.reshape(owners, -1) for value in vectors], axis=1)
+    room = -(-flat.shape[1] // 2048) * 2048
+    return jnp.pad(flat, ((0, 0), (0, room - flat.shape[1]))).reshape(owners, -1, 128)
+
+
+def plain_gather(stack, inner, outer, vectors):
+    owners = lax.axis_size("fsdp")
+    gathered = lax.all_gather(inner, "fsdp", axis=0, tiled=True)
+    return (
+        lax.all_gather(stack, "fsdp", axis=1, tiled=True),
+        gathered.reshape(W, 4, W).transpose(1, 0, 2),
+        lax.all_gather(outer, "fsdp", axis=0, tiled=True),
+        lax.all_gather(vectors, "fsdp", axis=0),
+    )
+
+
+def plain_reduce(stack, inner, outer, vectors):
+    def over_all(value, axis):
+        part = lax.psum_scatter(value, "fsdp", scatter_dimension=axis, tiled=True)
+        return lax.psum(part, "rep").astype(jnp.float32)
+
+    outer_part = over_all(outer, 0)
+    return (
+        over_all(stack, 1),
+        over_all(inner, 1),
+        outer_part.reshape(4, -1, W),
+        over_all(vectors, 0)[0],
+    )
+
 
 HEADS = 12
 HEAD_DIM = 64
-
-
 def layer_norm(value, gain, shift):
     mean = jnp.mean(value, axis=-1, keepdims=True)
     centered = value - mean
@@ -117,39 +521,28 @@
     norm_two_bias,
     out_grad,
 ):
+    owners = lax.axis_size("fsdp")
+    wide = owners == 8 and lax.axis_size("rep") == 4
+    part = w_query.shape[0]
+    small = pack_shard(
+        (
+            query_bias, value_bias, out_bias, norm_one_gain,
+            norm_one_bias, outer_bias, norm_two_gain, norm_two_bias, inner_bias,
+        ),
+        part,
+    )
+    gather, reduce = (gather_all, reduce_all) if wide else (plain_gather, plain_reduce)
+    weights, inner_blocks, outer_mat, vectors = gather(
+        jnp.stack([w_query, w_key, w_value, w_out]), w_inner, w_outer, small
+    )
+    query_mat, key_mat, value_mat, out_mat = weights
+    inner_mat = inner_blocks.transpose(1, 0, 2).reshape(W, 4 * W)
     (
-        query_mat,
-        key_mat,
-        value_mat,
-        out_mat,
-        query_shift,
-        value_shift,
-        out_shift,
-        gain_one,
-        shift_one,
-        inner_mat,
-        inner_shift,
-        outer_mat,
-        outer_shift,
-        gain_two,
-        shift_two,
-    ) = (
-        lax.all_gather(w_query, "fsdp", axis=0, tiled=True),
-        lax.all_gather(w_key, "fsdp", axis=0, tiled=True),
-        lax.all_gather(w_value, "fsdp", axis=0, tiled=True),
-        lax.all_gather(w_out, "fsdp", axis=0, tiled=True),
-        lax.all_gather(query_bias, "fsdp", axis=0, tiled=True),
-        lax.all_gather(value_bias, "fsdp", axis=0, tiled=True),
-        lax.all_gather(out_bias, "fsdp", axis=0, tiled=True),
-        lax.all_gather(norm_one_gain, "fsdp", axis=0, tiled=True),
-        lax.all_gather(norm_one_bias, "fsdp", axis=0, tiled=True),
-        lax.all_gather(w_inner, "fsdp", axis=0, tiled=True),
-        lax.all_gather(inner_bias, "fsdp", axis=0, tiled=True),
-        lax.all_gather(w_outer, "fsdp", axis=0, tiled=True),
-        lax.all_gather(outer_bias, "fsdp", axis=0, tiled=True),
-        lax.all_gather(norm_two_gain, "fsdp", axis=0, tiled=True),
-        lax.all_gather(norm_two_bias, "fsdp", axis=0, tiled=True),
-    )
+        query_shift, value_shift, out_shift, gain_one,
+        shift_one, outer_shift, gain_two, shift_two, inner_shift,
+    ) = unpack_full(vectors, part)
+    back_query, back_key, back_value, back_out = query_mat, key_mat, value_mat, out_mat
+    back_inner, back_outer = inner_mat, outer_mat
     seqs = doc_ids.shape[0]
     seg = doc_ids.shape[1]
     width = tokens.shape[1]
@@ -187,14 +580,6 @@
     second = normed + product(active_low, outer_mat) + outer_shift.astype(jnp.float32)
     output, norm_two_pull = jax.vjp(
         layer_norm, second, gain_two.astype(jnp.float32), shift_two.astype(jnp.float32)
-    )
-    back_query, back_key, back_value, back_out, back_inner, back_outer = (
-        lax.all_gather(w_query, "fsdp", axis=0, tiled=True),
-        lax.all_gather(w_key, "fsdp", axis=0, tiled=True),
-        lax.all_gather(w_value, "fsdp", axis=0, tiled=True),
-        lax.all_gather(w_out, "fsdp", axis=0, tiled=True),
-        lax.all_gather(w_inner, "fsdp", axis=0, tiled=True),
-        lax.all_gather(w_outer, "fsdp", axis=0, tiled=True),
     )
     grad_second, grad_gain_two, grad_shift_two = norm_two_pull(out_grad.astype(jnp.float32))
     grad_outer_low = grad_second.astype(jnp.bfloat16)
@@ -236,118 +621,39 @@
         .reshape(seqs * mem, width)
         .astype(jnp.bfloat16)
     )
+    low = jnp.bfloat16
+    stack_share, inner_share, outer_share, small_share = reduce(
+        jnp.stack([grad_w_query, grad_w_key, grad_w_value, grad_w_out]).astype(low),
+        grad_w_inner.astype(low).reshape(W, 4, W).transpose(1, 0, 2),
+        grad_w_outer.astype(low),
+        pack_full(
+            (
+                grad_query_bias, grad_value_bias, grad_out_bias, grad_gain_one,
+                grad_shift_one, grad_outer_bias, grad_gain_two, grad_shift_two, grad_inner_bias,
+            ),
+            owners,
+            part,
+        ),
+    )
     (
-        share_wq,
-        share_wk,
-        share_wv,
-        share_wo,
-        share_bq,
-        share_bv,
-        share_bo,
-        share_g1,
-        share_n1,
-        share_w1,
-        share_b1,
-        share_w2,
-        share_b2,
-        share_g2,
-        share_n2,
-    ) = (
-        lax.psum_scatter(
-            grad_w_query.astype(jnp.bfloat16), "fsdp", scatter_dimension=0, tiled=True
-        ).astype(jnp.float32),
-        lax.psum_scatter(
-            grad_w_key.astype(jnp.bfloat16), "fsdp", scatter_dimension=0, tiled=True
-        ).astype(jnp.float32),
-        lax.psum_scatter(
-            grad_w_value.astype(jnp.bfloat16), "fsdp", scatter_dimension=0, tiled=True
-        ).astype(jnp.float32),
-        lax.psum_scatter(
-            grad_w_out.astype(jnp.bfloat16), "fsdp", scatter_dimension=0, tiled=True
-        ).astype(jnp.float32),
-        lax.psum_scatter(
-            grad_query_bias.astype(jnp.bfloat16), "fsdp", scatter_dimension=0, tiled=True
-        ).astype(jnp.float32),
-        lax.psum_scatter(
-            grad_value_bias.astype(jnp.bfloat16), "fsdp", scatter_dimension=0, tiled=True
-        ).astype(jnp.float32),
-        lax.psum_scatter(
-            grad_out_bias.astype(jnp.bfloat16), "fsdp", scatter_dimension=0, tiled=True
-        ).astype(jnp.float32),
-        lax.psum_scatter(
-            grad_gain_one.astype(jnp.bfloat16), "fsdp", scatter_dimension=0, tiled=True
-        ).astype(jnp.float32),
-        lax.psum_scatter(
-            grad_shift_one.astype(jnp.bfloat16), "fsdp", scatter_dimension=0, tiled=True
-        ).astype(jnp.float32),
-        lax.psum_scatter(
-            grad_w_inner.astype(jnp.bfloat16), "fsdp", scatter_dimension=0, tiled=True
-        ).astype(jnp.float32),
-        lax.psum_scatter(
-            grad_inner_bias.astype(jnp.bfloat16), "fsdp", scatter_dimension=0, tiled=True
-        ).astype(jnp.float32),
-        lax.psum_scatter(
-            grad_w_outer.astype(jnp.bfloat16), "fsdp", scatter_dimension=0, tiled=True
-        ).astype(jnp.float32),
-        lax.psum_scatter(
-            grad_outer_bias.astype(jnp.bfloat16), "fsdp", scatter_dimension=0, tiled=True
-        ).astype(jnp.float32),
-        lax.psum_scatter(
-            grad_gain_two.astype(jnp.bfloat16), "fsdp", scatter_dimension=0, tiled=True
-        ).astype(jnp.float32),
-        lax.psum_scatter(
-            grad_shift_two.astype(jnp.bfloat16), "fsdp", scatter_dimension=0, tiled=True
-        ).astype(jnp.float32),
-    )
-    (
-        final_wq,
-        final_wk,
-        final_wv,
-        final_wo,
+        final_bq, final_bv, final_bo, final_g1, final_n1, final_b2, final_g2, final_n2, final_b1,
+    ) = unpack_full(small_share[None], part)
+    return (
+        output.astype(low),
+        grad_tokens,
+        grad_memory,
+        stack_share[0],
+        stack_share[1],
+        stack_share[2],
+        stack_share[3],
         final_bq,
         final_bv,
         final_bo,
         final_g1,
         final_n1,
-        final_w1,
+        inner_share.transpose(1, 0, 2).reshape(part, 4 * W),
         final_b1,
-        final_w2,
-        final_b2,
-        final_g2,
-        final_n2,
-    ) = (
-        lax.psum(share_wq.astype(jnp.bfloat16), "rep").astype(jnp.float32),
-        lax.psum(share_wk.astype(jnp.bfloat16), "rep").astype(jnp.float32),
-        lax.psum(share_wv.astype(jnp.bfloat16), "rep").astype(jnp.float32),
-        lax.psum(share_wo.astype(jnp.bfloat16), "rep").astype(jnp.float32),
-        lax.psum(share_bq.astype(jnp.bfloat16), "rep").astype(jnp.float32),
-        lax.psum(share_bv.astype(jnp.bfloat16), "rep").astype(jnp.float32),
-        lax.psum(share_bo.astype(jnp.bfloat16), "rep").astype(jnp.float32),
-        lax.psum(share_g1.astype(jnp.bfloat16), "rep").astype(jnp.float32),
-        lax.psum(share_n1.astype(jnp.bfloat16), "rep").astype(jnp.float32),
-        lax.psum(share_w1.astype(jnp.bfloat16), "rep").astype(jnp.float32),
-        lax.psum(share_b1.astype(jnp.bfloat16), "rep").astype(jnp.float32),
-        lax.psum(share_w2.astype(jnp.bfloat16), "rep").astype(jnp.float32),
-        lax.psum(share_b2.astype(jnp.bfloat16), "rep").astype(jnp.float32),
-        lax.psum(share_g2.astype(jnp.bfloat16), "rep").astype(jnp.float32),
-        lax.psum(share_n2.astype(jnp.bfloat16), "rep").astype(jnp.float32),
-    )
-    return (
-        output.astype(jnp.bfloat16),
-        grad_tokens,
-        grad_memory,
-        final_wq,
-        final_wk,
-        final_wv,
-        final_wo,
-        final_bq,
-        final_bv,
-        final_bo,
-        final_g1,
-        final_n1,
-        final_w1,
-        final_b1,
-        final_w2,
+        outer_share.reshape(4 * part, W),
         final_b2,
         final_g2,
         final_n2,

time: 930 us -> 578 us (0.62)
  waiting for transfers between devices: 416 us -> 0 us
  Pallas kernels: 0 us -> 175 us
  blocking collectives: 95.8 us -> 0 us
  local copies, waits for them, and re-layouts: 26.4 us -> 53 us
  matrix products: 269 us -> 251 us
  between operations: 17.1 us -> 1.85 us
  other arithmetic: 101 us -> 88.1 us
    reduce_scatter x6 -> x0, waiting for transfers between devices: 234 us -> none  [the longest x1 99.9 us: on_device(): lax.psum_scatter(grad_w_inner.astype(jnp.bfloat16), 'fsdp', scatter_dimen...]
    pallas_call x0 -> x2, Pallas kernels: none -> 175 us  [the longest x1 97.4 us: reduce_all(): pl.pallas_call(reduce_kernel, out_shape=(jax.ShapeDtypeStruct((4, part, W...]
    all_gather x6 -> x0, waiting for transfers between devices: 136 us -> none  [the longest x1 64.6 us: on_device(): lax.all_gather(w_inner, 'fsdp', axis=0, tiled=True)]
    unnamed x2 -> x0, blocking collectives: 60.3 us -> none
    psum x1 -> x0, waiting for transfers between devices: 42.3 us -> none  [on_device(): lax.psum(share_wq.astype(jnp.bfloat16), 'rep').astype(jnp.float32)]
    all_gather x1 -> x0, blocking collectives: 22.1 us -> none  [on_device(): lax.all_gather(inner_bias, 'fsdp', axis=0, tiled=True)]
    convert_element_type x23 -> x0, other arithmetic: 16.9 us -> none  [the longest x1 2.18 us: on_device(): lax.psum(share_w1.astype(jnp.bfloat16), 'rep').astype(jnp.float32)]
    psum x1 -> x0, blocking collectives: 13.4 us -> none  [on_device(): lax.psum(share_bq.astype(jnp.bfloat16), 'rep').astype(jnp.float32)]
  transfers between devices with their start and end apart: 13 -> 0, of which waited for: 8 -> 0; matrix products, arithmetic and copies ran while one was open for 35% -> 0% of each run, Pallas kernels for 0% -> 0%
where the time goes in v1:
time: 578 us; the launch traced here: 569 us
  matrix products  251 us (43%)
  Pallas kernels  175 us (30%)
  other arithmetic  88.1 us (15%)
  local copies, waits for them, and re-layouts  53 us (9%)
    pallas_call x1, Pallas kernels, reduce_all(): pl.pallas_call(reduce_kernel, out_shape=(jax.ShapeDtypeStruct((4, part, W...  97.4 us
    pallas_call x1, Pallas kernels, gather_all(): pl.pallas_call(gather_kernel, out_shape=(jax.ShapeDtypeStruct((4, W, W),...  77.9 us
    dot_general x6, matrix products, product(): return jnp.dot(left, right, preferred_element_type=jnp.float32)  52.5 us
    convert_element_type x1, other arithmetic, attend_backward(): grad_scores = (probs * (grad_probs - centre)).astype(jnp.bfloat16)  42.7 us
    dot_general x6, matrix products, against(): lax.dot_general(left, right, (((1,), (1,)), ((), ())), preferred_element_...  38.9 us
    dot_general x2, matrix products, attend_backward(): jnp.einsum('qhd,khd->hqk', grad_block, values, preferred_element_type=jnp...  36.5 us
    dot_general x6, matrix products, inner_rows(): lax.dot_general(left, right, (((0,), (0,)), ((), ())), preferred_element_...  30 us
    dot_general x2, matrix products, attend_backward(): jnp.einsum('hqk,qhd->khd', probs.astype(jnp.bfloat16), grad_block, prefer...  24.6 us

profile of v1, /device:TPU:1, one launch (start us, length us, event | category | flops | bytes accessed | tf_op | source)
XLA Modules:
  0.0 569.2 jit_solution(16075941851827726836)
XLA Ops:
  0.7 0.8 add_compare_fusion
  1.4 0.8 pad_add_fusion
  2.2 6.1 %concatenate.60 = bf16[1152]{0:T(1024)(128)(2,1)S(1)} concatenate(bf16[96]{0:T(256)(128)(2,1)} %param.26, bf16[96]{0:T(256)(128)(2,1)} %param.27, bf16[96]{0:T(256)(128)(2,1)} %param.28, bf16[96]{0:T(256)(128)(2,1)} %param.29, bf16[96]{0:T(256)(128)(2,1)} %param.30, bf16[96]{0:T(256)(128)(2,1)} %param.34, bf16[96]{0:T(256)(128)(2,1)} %param.35, bf16[96]{0:T(256)(128)(2,1)} %param.36, ...), dimensions={0} | concatenate | bytes 4608 | tf_op jit(solution)/shard_map/concatenate | solution.py:372
  8.9 0.8 pad_slice_fusion.1
  9.8 2.0 pad_maximum_fusion.5.a0
  11.8 1.0 or_or_fusion.1
  12.8 77.9 %gather_weights.1 = (bf16[4,768,768]{2,1,0:T(8,128)(2,1)}, bf16[4,768,768]{2,1,0:T(8,128)(2,1)}, bf16[3072,768]{1,0:T(8,128)(2,1)}, bf16[8,16,128]{2,1,0:T(8,128)(2,1)}) custom-call(bf16[4,96,768]{2,1,0:T(8,128)(2,1)} %pad_maximum_fusion.5.a0, bf16[96,3072]{1,0:T(8,128)(2,1)} %a1.1, bf16[384,768]{1,0:T(8,128)(2,1)} %a2.1, bf16[16,128]{1,0:T(8,128)(2,1)} %pad_bitcast_fusion.1.av), custom_call_target="tpu_custom_call" | custom-call | tf_op jit(solution)/shard_map/gather_weights/pallas_call | solution.py:152
  90.8 0.8 copy.47
  91.6 6.7 %copy.37 = bf16[768,4,768]{0,2,1:T(8,128)(2,1)} copy(bf16[768,4,768]{2,0,1:T(8,128)(2,1)} %bitcast.183) | data formatting | bytes 9437184 | tf_op jit(solution)/shard_map/transpose | solution.py:539
  100.7 3.3 add_convert_fusion.4
  104.4 1.5 add_convert_fusion.3
  106.0 1.4 convolution_convert_fusion.3
  107.4 10.7 %fusion.18 = (f32[12,512]{1,0:T(8,128)S(1)}, f32[12,512,1024]{2,1,0:T(8,128)}) fusion(pred[512,1024]{1,0:T(8,128)(4,1)S(1)} %get-tuple-element.126, bf16[512,12,64]{0,2,1:T(8,128)(2,1)S(1)} %bitcast.173, bf16[1024,12,64]{0,2,1:T(8,128)(2,1)S(1)} %bitcast.165), kind=kOutput, calls=%fused_computation.40 | convolution fusion | flops 824174592 | bytes 28073984 | tf_op jit(solution)/shard_map/while/body/eval_jaxpr/qhd,khd->hqk/dot_general | solution.py:445
  118.1 12.3 %fusion = f32[12,512]{1,0:T(8,128)S(1)} fusion(f32[12,512]{1,0:T(8,128)S(1)} %get-tuple-element.132, f32[12,512,1024]{2,1,0:T(8,128)} %get-tuple-element.133, pred[512,1024]{1,0:T(8,128)(4,1)S(1)} %get-tuple-element.126), kind=kLoop, calls=%fused_computation.12 | loop fusion | flops 25159680 | bytes 25739264 | tf_op jit(solution)/shard_map/while/body/eval_jaxpr/reduce_sum | solution.py:462
  131.0 2.5 copy-done
  133.5 8.9 %fusion.36 = bf16[12,64,512]{2,1,0:T(8,128)(2,1)} fusion(bf16[1024,12,64]{0,2,1:T(8,128)(2,1)S(1)} %bitcast.175, f32[12,512]{1,0:T(8,128)S(1)} %fusion, f32[12,512]{1,0:T(8,128)S(1)} %get-tuple-element.132, f32[12,512,1024]{2,1,0:T(8,128)S(1)} %copy-done, pred[512,1024]{1,0:T(8,128)(4,1)S(1)} %get-tuple-element.126), kind=kOutput, calls=%fused_computation.98 | convolution fusion | flops 837156864 | bytes 28098560 | tf_op jit(solution)/shard_map/while/body/eval_jaxpr/hqk,khd->qhd/dot_general | solution.py:464
  142.4 10.7 %fusion.19 = (f32[12,512]{1,0:T(8,128)S(1)}, f32[12,512,1024]{2,1,0:T(8,128)}) fusion(pred[512,1024]{1,0:T(8,128)(4,1)S(1)} %get-tuple-element.127, bf16[512,12,64]{0,2,1:T(8,128)(2,1)S(1)} %bitcast.171, bf16[1024,12,64]{0,2,1:T(8,128)(2,1)S(1)} %bitcast.166), kind=kOutput, calls=%fused_computation.41 | convolution fusion | flops 824174592 | bytes 28073984 | tf_op jit(solution)/shard_map/while/body/eval_jaxpr/qhd,khd->hqk/dot_general | solution.py:445
  153.1 12.3 %fusion.1 = f32[12,512]{1,0:T(8,128)S(1)} fusion(f32[12,512]{1,0:T(8,128)S(1)} %get-tuple-element.130, f32[12,512,1024]{2,1,0:T(8,128)} %get-tuple-element.131, pred[512,1024]{1,0:T(8,128)(4,1)S(1)} %get-tuple-element.127), kind=kLoop, calls=%fused_computation.13 | loop fusion | flops 25159680 | bytes 25739264 | tf_op jit(solution)/shard_map/while/body/eval_jaxpr/reduce_sum | solution.py:462
  166.1 2.5 copy-done.1
  168.5 7.8 %fusion.35 = bf16[12,64,512]{2,1,0:T(8,128)(2,1)S(1)} fusion(bf16[1024,12,64]{0,2,1:T(8,128)(2,1)S(1)} %bitcast.176, f32[12,512]{1,0:T(8,128)S(1)} %fusion.1, f32[12,512]{1,0:T(8,128)S(1)} %get-tuple-element.130, f32[12,512,1024]{2,1,0:T(8,128)S(1)} %copy-done.1, pred[512,1024]{1,0:T(8,128)(4,1)S(1)} %get-tuple-element.127), kind=kOutput, calls=%fused_computation.97 | convolution fusion | flops 837156864 | bytes 28098560 | tf_op jit(solution)/shard_map/while/body/eval_jaxpr/hqk,khd->qhd/dot_general | solution.py:464
  176.3 1.4 pad_maximum_fusion.2
  178.3 3.4 fusion.78
  182.3 37.5 %multiply_convert_fusion.2 = (bf16[1024,3072]{1,0:T(8,128)(2,1)S(1)}, f32[1024,3072]{1,0:T(8,128)}, f32[1024,3072]{1,0:T(8,128)}) fusion(f32[3072]{0:T(1024)S(1)} %reshape.518, bf16[768,3072]{0,1:T(8,128)(2,1)S(1)} %bitcast.182, f32[1024,768]{1,0:T(8,128)S(1)} %get-tuple-element.135, f32[768]{0:T(1024)S(1)} %reshape.517, f32[768]{0:T(1024)S(1)} %reshape.516, ...), kind=kOutput, calls=%fused_computation.24 | convolution fusion | flops 5043388416 | bytes 39348224 | tf_op jit(solution)/shard_map/dot_general | solution.py:424
  219.8 5.4 fusion.79
  225.8 0.9 copy-done.15
  226.6 1.2 fusion.23
  227.9 0.7 reshape.498
  228.5 0.7 reshape.499
  229.2 3.6 fusion.74
  233.2 17.1 %convert_reduce_fusion = (f32[3072]{0:T(1024)S(1)}, bf16[1024,3072]{1,0:T(8,128)(2,1)}) fusion(f32[1024,3072]{1,0:T(8,128)} %get-tuple-element.100, bf16[1024,768]{1,0:T(8,128)(2,1)S(1)} %get-tuple-element.92, bf16[3072,768]{1,0:T(8,128)(2,1)} %get-tuple-element.80, f32[1024,3072]{1,0:T(8,128)} %get-tuple-element.136, f32[3072]{0:T(1024)S(1)} %reshape.518), kind=kOutput, calls=%fused_computation.20 | convolution fusion | flops 4885312512 | bytes 37773312 | tf_op jit(solution)/shard_map/dot_general | solution.py:434
  250.2 9.9 %convolution_convert_fusion.g2 = bf16[3072,768]{1,0:T(8,128)(2,1)} fusion(bf16[1024,3072]{1,0:T(8,128)(2,1)} %copy-done.48, bf16[1024,768]{1,0:T(8,128)(2,1)S(1)} %get-tuple-element.92), kind=kOutput, calls=%fused_computation.42 | convolution fusion | flops 4834197504 | bytes 12582912 | tf_op jit(solution)/shard_map/dot_general | solution.py:428
  260.1 9.8 %multiply_reduce_fusion.2 = (f32[768]{0:T(1024)S(1)}, f32[1024]{0:T(1024)S(1)}, f32[768]{0:T(1024)S(1)}, f32[1024,768]{1,0:T(8,128)}) fusion(f32[1024,768]{1,0:T(8,128)S(1)} %copy-done.9, f32[1024]{0:T(1024)S(1)} %fusion.57, f32[1024]{0:T(1024)S(1)} %broadcast_multiply_fusion.1, f32[768]{0:T(1024)S(1)} %reshape.516, bf16[1024,3072]{1,0:T(8,128)(2,1)S(1)} %copy-done.46, ...), kind=kOutput, calls=%fused_computation.55 | convolution fusion | flops 4839699456 | bytes 20472832 | tf_op jit(solution)/shard_map/dot_general | solution.py:434
  270.1 3.7 fusion.73
  273.9 1.9 copy-done.47
  275.7 8.2 %convolution_convert_fusion.1 = bf16[768,3072]{1,0:T(8,128)(2,1)} fusion(bf16[1024,3072]{1,0:T(8,128)(2,1)S(1)} %copy-done.47, f32[1024,768]{1,0:T(8,128)S(1)} %copy-done.10, f32[768]{0:T(1024)S(1)} %reshape.517, f32[768]{0:T(1024)S(1)} %reshape.516, f32[1024]{0:T(1024)S(1)} %fusion.57, f32[1024]{0:T(1024)S(1)} %broadcast_multiply_fusion.1), kind=kOutput, calls=%fused_computation.43 | convolution fusion | flops 4838129664 | bytes 14170112 | tf_op jit(solution)/shard_map/dot_general | solution.py:428
  284.0 6.6 %copy.38 = bf16[768,3072]{0,1:T(8,128)(2,1)} copy(bf16[768,3072]{1,0:T(8,128)(2,1)} %convolution_convert_fusion.1) | data formatting | bytes 9437184 | tf_op jit(solution)/shard_map/convert_element_type | solution.py:627
  290.6 6.7 %copy.39 = bf16[768,4,768]{2,0,1:T(8,128)(2,1)} copy(bf16[768,4,768]{0,2,1:T(8,128)(2,1)} %bitcast.170) | data formatting | bytes 9437184 | tf_op jit(solution)/shard_map/reshape | solution.py:627
  297.7 1.3 copy-done.24
  299.0 2.4 fusion.34
  301.5 3.2 convolution_convert_fusion.2
  304.8 0.9 copy-done.21
  305.8 11.5 %fusion.5 = f32[12,64,1024]{2,1,0:T(8,128)S(1)} fusion(bf16[512,12,64]{0,2,1:T(8,128)(2,1)S(1)} %bitcast.192, f32[12,512]{1,0:T(8,128)S(1)} %copy-done.32, f32[12,512,1024]{2,1,0:T(8,128)} %get-tuple-element.131, pred[512,1024]{1,0:T(8,128)(4,1)S(1)} %copy-done.7), kind=kOutput, calls=%fused_computation.18 | convolution fusion | flops 830472192 | bytes 29646848 | tf_op jit(solution)/shard_map/while/body/eval_jaxpr/hqk,qhd->khd/dot_general | solution.py:478
  317.3 13.2 %convert_reduce_fusion.4 = (f32[12,64]{1,0:T(8,128)S(1)}, bf16[12,64,1024]{2,1,0:T(8,128)(2,1)}) fusion(f32[12,64,1024]{2,1,0:T(8,128)S(1)} %fusion.5, bf16[512,12,64]{0,2,1:T(8,128)(2,1)S(1)} %bitcast.194, f32[12,512]{1,0:T(8,128)S(1)} %copy-done.31, f32[12,512,1024]{2,1,0:T(8,128)} %get-tuple-element.133, pred[512,1024]{1,0:T(8,128)(4,1)S(1)} %copy-done.5), kind=kOutput, calls=%fused_computation.57 | convolution fusion | flops 833617152 | bytes 31222784 | tf_op jit(solution)/shard_map/while/body/eval_jaxpr/hqk,qhd->khd/dot_general | solution.py:478
  330.5 4.3 fusion.33
  334.9 18.2 %multiply_reduce_fusion.1 = (f32[12,512]{1,0:T(8,128)S(1)}, f32[12,512,1024]{2,1,0:T(8,128)}) fusion(f32[12,512]{1,0:T(8,128)S(1)} %copy-done.31, f32[12,512,1024]{2,1,0:T(8,128)} %get-tuple-element.133, pred[512,1024]{1,0:T(8,128)(4,1)} %copy-done.4, bf16[512,12,64]{0,2,1:T(8,128)(2,1)} %bitcast.195, bf16[1024,12,64]{0,2,1:T(8,128)(2,1)} %bitcast.177), kind=kOutput, calls=%fused_computation.4 | convolution fusion | flops 836757504 | bytes 53264384 | tf_op jit(solution)/shard_map/while/body/eval_jaxpr/qhd,khd->hqk/dot_general | solution.py:484
  353.1 18.2 %multiply_reduce_fusion = (f32[12,512]{1,0:T(8,128)S(1)}, f32[12,512,1024]{2,1,0:T(8,128)}) fusion(f32[12,512]{1,0:T(8,128)S(1)} %copy-done.32, f32[12,512,1024]{2,1,0:T(8,128)} %get-tuple-element.131, pred[512,1024]{1,0:T(8,128)(4,1)} %copy-done.6, bf16[512,12,64]{0,2,1:T(8,128)(2,1)} %bitcast.193, bf16[1024,12,64]{0,2,1:T(8,128)(2,1)} %bitcast.178), kind=kOutput, calls=%fused_computation.1 | convolution fusion | flops 836757504 | bytes 53264384 | tf_op jit(solution)/shard_map/while/body/eval_jaxpr/qhd,khd->hqk/dot_general | solution.py:484
  371.3 42.7 %multiply_convert_fusion = (bf16[12,512,1024]{2,1,0:T(8,128)(2,1)}, bf16[12,512,1024]{2,1,0:T(8,128)(2,1)}) fusion(f32[12,512,1024]{2,1,0:T(8,128)} %get-tuple-element.143, f32[12,512]{1,0:T(8,128)S(1)} %get-tuple-element.142, f32[12,512]{1,0:T(8,128)S(1)} %copy-done.32, f32[12,512,1024]{2,1,0:T(8,128)} %get-tuple-element.131, pred[512,1024]{1,0:T(8,128)(4,1)} %copy-done.6, ...), kind=kLoop, calls=%fused_computation | loop fusion | flops 75497472 | bytes 126976000 | tf_op jit(solution)/shard_map/while/body/eval_jaxpr/convert_element_type | solution.py:488
  414.1 9.5 %multiply_convert_fusion.4 = bf16[12,64,512]{2,1,0:T(8,128)(2,1)} fusion(bf16[1024,12,64]{0,2,1:T(8,128)(2,1)S(1)} %bitcast.168, bf16[12,512,1024]{2,1,0:T(8,128)(2,1)} %get-tuple-element.148), kind=kOutput, calls=%fused_computation.86 | convolution fusion | flops 806092800 | bytes 14942208 | tf_op jit(solution)/shard_map/while/body/eval_jaxpr/hqk,khd->qhd/dot_general | solution.py:490
  423.6 10.1 %multiply_convert_fusion.5 = bf16[12,64,512]{2,1,0:T(8,128)(2,1)} fusion(bf16[1024,12,64]{0,2,1:T(8,128)(2,1)} %bitcast.167, bf16[12,512,1024]{2,1,0:T(8,128)(2,1)} %get-tuple-element.149), kind=kOutput, calls=%fused_computation.87 | convolution fusion | flops 806092800 | bytes 14942208 | tf_op jit(solution)/shard_map/while/body/eval_jaxpr/hqk,khd->qhd/dot_general | solution.py:490
  433.7 7.3 %fusion.80 = f32[12,64,1024]{2,1,0:T(8,128)S(1)} fusion(bf16[512,12,64]{0,2,1:T(8,128)(2,1)} %bitcast.174, bf16[12,512,1024]{2,1,0:T(8,128)(2,1)} %get-tuple-element.149), kind=kOutput, calls=%fused_computation.183 | convolution fusion | flops 805306368 | bytes 16515072 | tf_op jit(solution)/shard_map/while/body/eval_jaxpr/hqk,qhd->khd/dot_general | solution.py:495
  441.0 3.5 multiply_convert_fusion.3
  445.7 3.4 fusion.31
  449.1 1.7 fusion.32
  450.9 2.5 pad_maximum_fusion.g0
  453.3 97.4 %reduce_gradients.1 = (f32[4,96,768]{2,1,0:T(8,128)}, f32[4,96,768]{2,1,0:T(8,128)}, f32[4,96,768]{2,1,0:T(8,128)}, f32[16,128]{1,0:T(8,128)}) custom-call(bf16[4,768,768]{2,1,0:T(8,128)(2,1)} %pad_maximum_fusion.g0, bf16[4,768,768]{2,1,0:T(8,128)(2,1)} %bitcast.169, bf16[3072,768]{1,0:T(8,128)(2,1)} %convolution_convert_fusion.g2, f32[8,16,128]{2,1,0:T(8,128)} %bitcast.206), custom_call_target="tpu_custom_call" | custom-call | tf_op jit(solution)/shard_map/reduce_gradients/pallas_call | solution.py:332
  550.7 2.4 slice_bitcast_fusion
  553.1 1.2 slice_reduce_fusion
  554.3 1.4 slice_bitcast_fusion.4
  555.7 1.1 copy.41
  556.8 2.8 fusion.39
  559.7 2.8 fusion.42
  562.5 3.2 add_bitcast_fusion
  566.3 1.4 fusion.30
  567.7 1.0 copy.49
  (153 shorter events, 9.5 us)
Async XLA Ops:
  12.8 118.2 %copy-start.4 = (pred[512,1024]{1,0:T(8,128)(4,1)}, pred[512,1024]{1,0:T(8,128)(4,1)S(1)}, u32[]{:S(2)}) copy-start(pred[512,1024]{1,0:T(8,128)(4,1)S(1)} %get-tuple-element.126) | copy-start | bytes 1572868
  12.8 153.2 %copy-start.6 = (pred[512,1024]{1,0:T(8,128)(4,1)}, pred[512,1024]{1,0:T(8,128)(4,1)S(1)}, u32[]{:S(2)}) copy-start(pred[512,1024]{1,0:T(8,128)(4,1)S(1)} %get-tuple-element.127) | copy-start | bytes 1572868
  91.6 9.2 %copy-start.44 = (bf16[10,768]{1,0:T(8,128)(2,1)S(1)}, bf16[10,768]{1,0:T(8,128)(2,1)}, u32[]{:S(2)}) copy-start(bf16[10,768]{1,0:T(8,128)(2,1)} %param.20) | copy-start | bytes 46084
  100.7 3.4 copy-start.33
  100.7 3.6 copy-start.41
  104.1 62.0 %copy-start.14 = (bf16[1024,768]{0,1:T(8,128)(2,1)}, bf16[1024,768]{0,1:T(8,128)(2,1)S(1)}, u32[]{:S(2)}) copy-start(bf16[1024,768]{0,1:T(8,128)(2,1)S(1)} %add_convert_fusion.4) | copy-start | bytes 4718596
  105.9 1.5 copy-start.13
  106.0 36.5 %copy-start.11 = (bf16[512,768]{0,1:T(8,128)(2,1)}, bf16[512,768]{0,1:T(8,128)(2,1)S(1)}, u32[]{:S(2)}) copy-start(bf16[512,768]{0,1:T(8,128)(2,1)S(1)} %get-tuple-element.105) | copy-start | bytes 2359300
  107.4 35.0 %copy-start.2 = (bf16[1024,768]{0,1:T(8,128)(2,1)}, bf16[1024,768]{0,1:T(8,128)(2,1)S(1)}, u32[]{:S(2)}) copy-start(bf16[1024,768]{0,1:T(8,128)(2,1)S(1)} %convolution_convert_fusion.3) | copy-start | bytes 4718596
  118.1 15.4 %copy-start = (f32[12,512,1024]{2,1,0:T(8,128)S(1)}, f32[12,512,1024]{2,1,0:T(8,128)}, u32[]{:S(2)}) copy-start(f32[12,512,1024]{2,1,0:T(8,128)} %get-tuple-element.133) | copy-start | bytes 75497472
  153.1 15.4 %copy-start.1 = (f32[12,512,1024]{2,1,0:T(8,128)S(1)}, f32[12,512,1024]{2,1,0:T(8,128)}, u32[]{:S(2)}) copy-start(f32[12,512,1024]{2,1,0:T(8,128)} %get-tuple-element.131) | copy-start | bytes 75497472
  168.5 7.8 %copy-start.30 = (bf16[12,64,512]{2,1,0:T(8,128)(2,1)S(1)}, bf16[12,64,512]{2,1,0:T(8,128)(2,1)}, u32[]{:S(2)}) copy-start(bf16[12,64,512]{2,1,0:T(8,128)(2,1)} %fusion.36) | copy-start | bytes 2359300
  176.3 2.0 copy-start.42
  177.7 4.5 slice-start.3
  178.3 4.0 slice-start.4
  178.3 41.5 %slice-start.5 = ((s8[4718592]{0:T(1024)(128)(4,1)}), s8[4194304]{0:T(1024)(128)(4,1)S(1)}, s32[]{:S(2)}) async-start(s8[4718592]{0:T(1024)(128)(4,1)} %bitcast.222), calls=%async_computation.5 | async-start | bytes 8388608
  181.7 38.1 %copy-start.8 = (f32[1024,768]{1,0:T(8,128)}, f32[1024,768]{1,0:T(8,128)S(1)}, u32[]{:S(2)}) copy-start(f32[1024,768]{1,0:T(8,128)S(1)} %get-tuple-element.135) | copy-start | bytes 9437188
  182.2 37.6 %copy-start.35 = (f32[1024]{0:T(1024)}, f32[1024]{0:T(1024)S(1)}, u32[]{:S(2)}) copy-start(f32[1024]{0:T(1024)S(1)} %multiply_reduce_fusion.5) | copy-start | bytes 12292
  182.3 37.5 %copy-start.40 = (f32[768]{0:T(1024)S(1)}, f32[768]{0:T(1024)}, u32[]{:S(2)}) copy-start(f32[768]{0:T(1024)} %reshape.519) | copy-start | bytes 9220
  182.3 37.5 %slice-start.6 = ((s8[4718592]{0:T(1024)(128)(4,1)}), s8[524288]{0:T(1024)(128)(4,1)S(1)}, s32[]{:S(2)}) async-start(s8[4718592]{0:T(1024)(128)(4,1)} %bitcast.222), calls=%async_computation.6 | async-start | bytes 1048576
  219.8 5.4 copy-start.48
  225.2 1.4 copy-start.15
  225.2 1.4 copy-start.34
  225.7 3.5 copy-start.37
  250.2 9.9 %copy-start.9 = (f32[1024,768]{1,0:T(8,128)S(1)}, f32[1024,768]{1,0:T(8,128)}, u32[]{:S(2)}) copy-start(f32[1024,768]{1,0:T(8,128)} %copy-done.8) | copy-start | bytes 9437188
  250.2 9.9 %copy-start.46 = (bf16[1024,3072]{1,0:T(8,128)(2,1)S(1)}, bf16[1024,3072]{1,0:T(8,128)(2,1)}, u32[]{:S(2)}) copy-start(bf16[1024,3072]{1,0:T(8,128)(2,1)} %get-tuple-element.147) | copy-start | bytes 18874372
  260.1 9.9 %copy-start.36 = (f32[1024]{0:T(1024)S(1)}, f32[1024]{0:T(1024)}, u32[]{:S(2)}) copy-start(f32[1024]{0:T(1024)} %copy-done.35) | copy-start | bytes 12292
  270.1 3.8 copy-start.10
  270.1 5.6 copy-start.47
  297.3 1.7 copy-start.24
  297.7 3.8 copy-start.25
  304.7 1.1 copy-start.7
  304.7 1.1 copy-start.32
  304.8 0.9 copy-start.21
  304.8 12.4 %copy-start.22 = (bf16[512,768]{0,1:T(8,128)(2,1)}, bf16[512,768]{0,1:T(8,128)(2,1)S(1)}, u32[]{:S(2)}) copy-start(bf16[512,768]{0,1:T(8,128)(2,1)S(1)} %get-tuple-element.103) | copy-start | bytes 2359300
  305.7 11.5 %copy-start.5 = (pred[512,1024]{1,0:T(8,128)(4,1)S(1)}, pred[512,1024]{1,0:T(8,128)(4,1)}, u32[]{:S(2)}) copy-start(pred[512,1024]{1,0:T(8,128)(4,1)} %copy-done.4) | copy-start | bytes 1572868
  305.7 11.5 %copy-start.31 = (f32[12,512]{1,0:T(8,128)S(1)}, f32[12,512]{1,0:T(8,128)}, u32[]{:S(2)}) copy-start(f32[12,512]{1,0:T(8,128)} %log_add_fusion.1) | copy-start | bytes 73732
  317.2 13.3 %copy-start.45 = (bf16[10,768]{1,0:T(8,128)(2,1)S(1)}, bf16[10,768]{1,0:T(8,128)(2,1)}, u32[]{:S(2)}) copy-start(bf16[10,768]{1,0:T(8,128)(2,1)} %param.20) | copy-start | bytes 46084
  371.3 42.8 %copy-start.3 = (bf16[1024,768]{0,1:T(8,128)(2,1)S(1)}, bf16[1024,768]{0,1:T(8,128)(2,1)}, u32[]{:S(2)}) copy-start(bf16[1024,768]{0,1:T(8,128)(2,1)} %copy-done.2) | copy-start | bytes 4718596
  423.6 17.3 %slice-start = ((s8[12582912]{0:T(1024)(128)(4,1)}), s8[4194304]{0:T(1024)(128)(4,1)S(1)}, s32[]{:S(2)}) async-start(s8[12582912]{0:T(1024)(128)(4,1)} %bitcast.163), calls=%async_computation | async-start | bytes 8388608
  423.6 17.4 %slice-start.1 = ((s8[12582912]{0:T(1024)(128)(4,1)}), s8[4194304]{0:T(1024)(128)(4,1)S(1)}, s32[]{:S(2)}) async-start(s8[12582912]{0:T(1024)(128)(4,1)} %bitcast.163), calls=%async_computation.1 | async-start | bytes 8388608
  433.7 7.3 %slice-start.2 = ((s8[12582912]{0:T(1024)(128)(4,1)}), s8[4194304]{0:T(1024)(128)(4,1)S(1)}, s32[]{:S(2)}) async-start(s8[12582912]{0:T(1024)(128)(4,1)} %bitcast.163), calls=%async_computation.2 | async-start | bytes 8388608
  433.7 7.3 %copy-start.12 = (bf16[512,768]{0,1:T(8,128)(2,1)S(1)}, bf16[512,768]{0,1:T(8,128)(2,1)}, u32[]{:S(2)}) copy-start(bf16[512,768]{0,1:T(8,128)(2,1)} %copy-done.11) | copy-start | bytes 2359300
  441.0 3.6 copy-start.17
  441.0 3.6 copy-start.19
  441.0 3.9 copy-start.38
  441.0 3.9 copy-start.39
  445.7 3.4 copy-start.16
  445.7 3.4 copy-start.43
  449.1 1.7 copy-start.26
  449.1 1.7 copy-start.27
  550.7 4.9 copy-start.29
  556.8 2.8 copy-start.18
  556.8 2.8 copy-start.20
  559.7 2.8 copy-start.23
  565.7 2.0 copy-start.28
